TPU v7x, 16 devices: a whole 2x2x2 slice. The times are simulated.
16 devices in a mesh: ep: 16 (over z, y, x, core).
Axes of the slice: x: 2, y: 2, z: 2, core: 2. Of those that a mesh axis runs over, the one named last changes fastest.
Arguments:
- tokens: bfloat16 [256, 256, 1024], P('ep')
- pad_mask: int32 [256, 256], P('ep')
- second_draw: float32 [256, 256], P('ep')
- choices: int32 [256, 256, 2], P('ep')
- norm_attn: float32 [1024], replicated
- w_query: bfloat16 [1024, 16, 64], replicated
- w_key: bfloat16 [1024, 16, 64], replicated
- w_value: bfloat16 [1024, 16, 64], replicated
- w_attn_out: bfloat16 [16, 64, 1024], replicated
- norm_moe: float32 [1024], replicated
- w_gate: float32 [1024, 32], replicated
- w_in: bfloat16 [32, 1024, 2816], P('ep')
- w_out: bfloat16 [32, 2816, 1024], P('ep')
Outputs:
- output 1: bfloat16 [256, 256, 1024], P('ep')
- output 2: float32 [], replicated
All inputs are finite; a program needn't handle non-finite values.
Results may differ from a plain program's by a relative error of at most 0.02.
Values are sent between devices in bfloat16 or wider.
A program may use at most 1 GiB of HBM per device.

v0:
```python
import jax
import jax.numpy as jnp
from jax import lax
from jax.sharding import PartitionSpec as P, NamedSharding

NORM_EPS = 1e-6


def rms_norm(values, scale_vec):
    values_f = values.astype(jnp.float32)
    inv_rms = lax.rsqrt(jnp.mean(values_f * values_f, axis=-1, keepdims=True) + NORM_EPS)
    return (values_f * inv_rms * scale_vec).astype(jnp.bfloat16)


def attention_block(tokens, pad_mask, norm_attn, w_query, w_key, w_value, w_attn_out):
    normed = rms_norm(tokens, norm_attn)
    q_heads = jnp.einsum("gsd,dhc->gshc", normed, w_query, preferred_element_type=jnp.float32).astype(jnp.bfloat16)
    k_heads = jnp.einsum("gsd,dhc->gshc", normed, w_key, preferred_element_type=jnp.float32).astype(jnp.bfloat16)
    v_heads = jnp.einsum("gsd,dhc->gshc", normed, w_value, preferred_element_type=jnp.float32).astype(jnp.bfloat16)
    head_scale = q_heads.shape[-1] ** -0.5
    scores = jnp.einsum("gqhc,gkhc->ghqk", q_heads, k_heads, preferred_element_type=jnp.float32) * head_scale
    scores = jnp.where(pad_mask[:, None, None, :] == 1, scores, -1e30)
    attn_probs = jax.nn.softmax(scores, axis=-1).astype(jnp.bfloat16)
    context = jnp.einsum("ghqk,gkhc->gqhc", attn_probs, v_heads, preferred_element_type=jnp.float32).astype(jnp.bfloat16)
    attn_out = jnp.einsum("gqhc,hcd->gqd", context, w_attn_out, preferred_element_type=jnp.float32)
    return (tokens.astype(jnp.float32) + attn_out).astype(jnp.bfloat16)


def gate_tokens(moe_in, pad_mask, second_draw, choices, w_gate, capacity):
    seq_len = moe_in.shape[1]
    expert_ids = jnp.arange(w_gate.shape[1])
    logits = jnp.einsum("gsd,de->gse", moe_in, w_gate, precision=lax.Precision.HIGHEST, preferred_element_type=jnp.float32)
    gate_probs = jax.nn.softmax(logits, axis=-1)
    is_valid = pad_mask == 1
    first_hot = choices[:, :, 0:1] == expert_ids
    second_hot = choices[:, :, 1:2] == expert_ids
    p_first = jnp.sum(jnp.where(first_hot, gate_probs, 0.0), axis=-1)
    p_second = jnp.sum(jnp.where(second_hot, gate_probs, 0.0), axis=-1)
    gate_first = p_first / (p_first + p_second)
    gate_second = p_second / (p_first + p_second)
    want_second = is_valid & (second_draw < 2.0 * gate_second)
    first_take = (first_hot & is_valid[:, :, None]).astype(jnp.int32)
    first_pos = jnp.sum((jnp.cumsum(first_take, axis=1) - 1) * first_take, axis=-1)
    first_count = jnp.sum(first_take, axis=1)
    keep_first = is_valid & (first_pos < capacity)
    second_take = (second_hot & want_second[:, :, None]).astype(jnp.int32)
    second_pos = jnp.sum((jnp.cumsum(second_take, axis=1) - 1 + jnp.minimum(first_count, capacity)[:, None, :]) * second_take, axis=-1)
    keep_second = want_second & (second_pos < capacity)
    density = jnp.sum(jnp.where(is_valid[:, :, None], gate_probs, 0.0), axis=1) / seq_len
    aux_sum = jnp.sum(first_count.astype(jnp.float32) / seq_len * density)
    return gate_first, gate_second, first_pos, second_pos, keep_first, keep_second, aux_sum


def build_tensors(choices, gate_first, gate_second, first_pos, second_pos, keep_first, keep_second, experts, capacity):
    expert_ids = jnp.arange(experts)
    slot_ids = jnp.arange(capacity)
    first_slot = (first_pos[:, :, None] == slot_ids) & keep_first[:, :, None]
    second_slot = (second_pos[:, :, None] == slot_ids) & keep_second[:, :, None]
    first_mask = (choices[:, :, 0:1] == expert_ids)[:, :, :, None] & first_slot[:, :, None, :]
    second_mask = (choices[:, :, 1:2] == expert_ids)[:, :, :, None] & second_slot[:, :, None, :]
    dispatch = (first_mask | second_mask).astype(jnp.bfloat16)
    combine = (jnp.where(first_mask, gate_first[:, :, None, None], 0.0) + jnp.where(second_mask, gate_second[:, :, None, None], 0.0)).astype(jnp.bfloat16)
    return dispatch, combine


def solution(mesh):
    n_dev = mesh.shape["ep"]

    def local_step(tokens, pad_mask, second_draw, choices, norm_attn, w_query, w_key, w_value, w_attn_out, norm_moe, w_gate, w_in, w_out):
        groups_local = tokens.shape[0]
        seq_len = tokens.shape[1]
        experts = w_gate.shape[1]
        capacity = (2 * seq_len + experts - 1) // experts
        hidden = attention_block(tokens, pad_mask, norm_attn, w_query, w_key, w_value, w_attn_out)
        moe_in = rms_norm(hidden, norm_moe)
        gate_first, gate_second, first_pos, second_pos, keep_first, keep_second, aux_sum = gate_tokens(moe_in, pad_mask, second_draw, choices, w_gate, capacity)
        dispatch, combine = build_tensors(choices, gate_first, gate_second, first_pos, second_pos, keep_first, keep_second, experts, capacity)
        send_buf = jnp.einsum("gsec,gsd->egcd", dispatch, moe_in, preferred_element_type=jnp.float32).astype(jnp.bfloat16)
        received = lax.all_to_all(send_buf, "ep", 0, 1, tiled=True)
        inner_act = jnp.maximum(jnp.einsum("egcd,edf->egcf", received, w_in, preferred_element_type=jnp.float32), 0.0).astype(jnp.bfloat16)
        expert_out = jnp.einsum("egcf,efd->egcd", inner_act, w_out, preferred_element_type=jnp.float32).astype(jnp.bfloat16)
        returned = lax.all_to_all(expert_out, "ep", 1, 0, tiled=True)
        moe_out = jnp.einsum("gsec,egcd->gsd", combine, returned, preferred_element_type=jnp.float32)
        out_tokens = (hidden.astype(jnp.float32) + moe_out).astype(jnp.bfloat16)
        aux_loss = lax.psum(aux_sum, "ep") * experts / (groups_local * n_dev)
        return out_tokens, aux_loss

    by_group = P("ep")
    replicated = P()
    in_specs = (by_group, by_group, by_group, by_group, replicated, replicated, replicated, replicated, replicated, replicated, replicated, by_group, by_group)
    return jax.shard_map(local_step, mesh=mesh, in_specs=in_specs, out_specs=(by_group, replicated), check_vma=False)
```

profile of v0, /device:TPU:0, one launch (start us, length us, event | category | flops | bytes accessed | tf_op | source)
XLA Modules:
  0.0 908.2 jit_solution(12732649428442705097)
XLA Ops:
  0.6 0.0 copy-start
  0.6 5.2 fusion.8
  5.9 0.7 broadcast_compare_fusion
  6.6 0.6 and.94
  7.2 14.2 %fusion.126 = bf16[16,256,16,64]{1,3,2,0:T(8,128)(2,1)} fusion(bf16[16,256,1024]{2,1,0:T(8,128)(2,1)} %param.13, f32[1024]{0:T(1024)} %param.17, f32[16,256]{1,0:T(8,128)S(1)} %add_rsqrt_fusion.1, bf16[1024,16,64]{0,2,1:T(8,128)(2,1)} %param.18), kind=kOutput, calls=%fused_computation.44.clone.2 | convolution fusion | flops 8610906112 | bytes 18894848 | tf_op jit(solution)/shard_map/gsd,dhc->gshc/dot_general | solution.py:17
  21.4 31.6 %fusion.29 = f32[16,16,256,256]{2,3,1,0:T(8,128)} fusion(bf16[16,256,1024]{2,1,0:T(8,128)(2,1)} %param.13, f32[1024]{0:T(1024)S(1)} %copy-done.2, f32[16,256]{1,0:T(8,128)S(1)} %add_rsqrt_fusion.1, bf16[1024,16,64]{0,2,1:T(8,128)(2,1)S(1)} %copy-done, bf16[16,256,16,64]{1,3,2,0:T(8,128)(2,1)} %fusion.126), kind=kOutput, calls=%fused_computation.41 | convolution fusion | flops 10758389760 | bytes 86003712 | tf_op jit(solution)/shard_map/gqhc,gkhc->ghqk/dot_general | solution.py:21
  53.0 68.7 %fusion.90 = (f32[16,16,256]{2,1,0:T(8,128)S(1)}, f32[16,16,256,256]{2,3,1,0:T(8,128)}) fusion(f32[16,16,256,256]{2,3,1,0:T(8,128)} %fusion.29, pred[16,256]{1,0:T(8,128)(4,1)S(1)} %broadcast_compare_fusion), kind=kOutput, calls=%fused_computation.116 | output fusion | flops 100663552 | bytes 134483968 | tf_op jit(solution)/shard_map/sub | solution.py:23
  121.7 14.8 %fusion.56 = bf16[16,256,16,64]{1,3,2,0:T(8,128)(2,1)} fusion(bf16[16,256,1024]{2,1,0:T(8,128)(2,1)} %param.13, f32[1024]{0:T(1024)S(1)} %copy-done.2, f32[16,256]{1,0:T(8,128)S(1)} %add_rsqrt_fusion.1, bf16[1024,16,64]{0,2,1:T(8,128)(2,1)S(1)} %copy-done.25), kind=kOutput, calls=%fused_computation.59 | convolution fusion | flops 8606711808 | bytes 18894848 | tf_op jit(solution)/shard_map/gsd,dhc->gshc/dot_general | solution.py:19
  136.5 27.7 %fusion.27.clone.4 = bf16[16,256,16,64]{1,3,2,0:T(8,128)(2,1)} fusion(f32[16,16,256,256]{2,3,1,0:T(8,128)} %get-tuple-element.13, f32[16,16,256]{2,1,0:T(8,128)S(1)} %get-tuple-element.12, bf16[16,256,16,64]{1,3,2,0:T(8,128)(2,1)} %fusion.56), kind=kOutput, calls=%fused_computation.39.clone.clone.clone.1 | convolution fusion | flops 2185232384 | bytes 84148224 | tf_op jit(solution)/shard_map/ghqk,gkhc->gqhc/dot_general | solution.py:24
  164.3 15.7 %fusion.12 = (f32[16,256]{1,0:T(8,128)S(1)}, bf16[16,256,1024]{2,1,0:T(8,128)(2,1)S(1)}) fusion(bf16[16,64,1024]{2,1,0:T(8,128)(2,1)} %param.21, bf16[16,256,1024]{2,1,0:T(8,128)(2,1)} %param.13, bf16[16,256,16,64]{1,3,2,0:T(8,128)(2,1)} %fusion.27.clone.4), kind=kOutput, calls=%fused_computation.22 | convolution fusion | flops 8615096320 | bytes 27279360 | tf_op jit(solution)/shard_map/gqhc,hcd->gqd/dot_general | solution.py:25
  180.0 0.0 copy-start.28
  180.1 0.1 iota_compare_fusion.1
  180.2 0.1 iota_compare_fusion.3
  180.3 3.1 copy-done.28
  183.4 0.0 copy-done.26
  183.4 7.4 fusion.37
  190.8 0.0 copy-done.19
  190.8 1.0 select_reduce_fusion
  191.9 0.1 fusion.73
  192.0 9.2 %reduce-window.14 = s32[16,32,2,128]{3,1,2,0:T(8,128)S(1)} reduce-window(s32[16,32,2,128]{3,1,2,0:T(8,128)S(1)} %fusion.73, s32[]{:T(128)} %constant.40.clone.1), window={size=1x1x1x128 pad=0_0x0_0x0_0x127_0}, to_apply=%region_3.4 | reduce-window | flops 16646144 | bytes 1048580 | tf_op jit(solution)/shard_map/reduce-window
  201.2 0.2 slice.26
  201.4 0.3 copy.43
  201.7 0.1 fusion.81
  201.8 0.5 fusion.71
  202.3 0.6 fusion.83
  202.9 0.1 fusion.76
  203.0 0.1 fusion.75
  203.1 9.2 %reduce-window.16 = s32[16,32,2,128]{3,1,2,0:T(8,128)S(1)} reduce-window(s32[16,32,2,128]{3,1,2,0:T(8,128)S(1)} %fusion.75, s32[]{:T(128)} %constant.40.clone.1), window={size=1x1x1x128 pad=0_0x0_0x0_0x127_0}, to_apply=%region_11.12 | reduce-window | flops 16646144 | bytes 1048580 | tf_op jit(solution)/shard_map/reduce-window.2
  212.3 0.2 slice.28
  212.6 0.3 copy.47
  212.8 0.1 fusion.79
  212.9 0.3 fusion.69
  213.3 0.1 fusion.77
  213.4 10.7 %convert_bitcast_fusion = bf16[32,16,16,1024]{3,0,2,1:T(8,128)(2,1)} fusion(bf16[16,256,1024]{2,1,0:T(8,128)(2,1)} %copy-done.28, f32[1024]{0:T(1024)S(1)} %copy-done.27, f32[16,256]{1,0:T(8,128)S(1)} %add_rsqrt_fusion, pred[16,256,16]{1,2,0:T(8,128)(4,1)S(1)} %fusion.77, pred[16,256,32]{1,2,0:T(8,128)(4,1)S(1)} %iota_compare_fusion.1, ...), kind=kOutput, calls=%fused_computation.28 | convolution fusion | flops 4326424576 | bytes 25579520 | tf_op jit(solution)/shard_map/gsec,gsd->egcd/dot_general | solution.py:78
  224.1 15.4 %copy.50 = bf16[32,16,16,1024]{3,2,1,0:T(8,128)(2,1)S(1)} copy(bf16[32,16,16,1024]{3,0,2,1:T(8,128)(2,1)} %convert_bitcast_fusion) | data formatting | bytes 33554432 | tf_op jit(solution)/shard_map/convert_element_type | solution.py:78
  239.5 194.2 %all_to_all.36 = bf16[32,16,16,1024]{3,2,1,0:T(8,128)(2,1)S(1)} all-to-all(bf16[32,16,16,1024]{3,2,1,0:T(8,128)(2,1)S(1)} %copy.50), channel_id=1, replica_groups=mesh['ep'=16] {'ep'}, dimensions={0} | all-to-all | bytes 33554432 | tf_op jit(solution)/shard_map/all_to_all | solution.py:79
  433.6 6.7 copy.51
  440.3 72.1 %maximum_convert_fusion.clone.4 = bf16[2,256,16,2816]{3,1,2,0:T(8,128)(2,1)} fusion(bf16[2,256,16,1024]{3,2,1,0:T(8,128)(2,1)} %bitcast.144, bf16[2,1024,2816]{2,1,0:T(8,128)(2,1)} %param.24), kind=kOutput, calls=%fused_computation.3.clone.clone.clone.1 | convolution fusion | flops 47290777600 | bytes 74448896 | tf_op jit(solution)/shard_map/egcd,edf->egcf/dot_general | solution.py:80
  512.4 56.8 %convolution_convert_fusion = bf16[2,256,16,1024]{3,1,2,0:T(8,128)(2,1)} fusion(bf16[2,2816,1024]{2,1,0:T(8,128)(2,1)} %param.25, bf16[2,256,16,2816]{3,1,2,0:T(8,128)(2,1)} %maximum_convert_fusion.clone.4), kind=kOutput, calls=%fused_computation.29 | convolution fusion | flops 47253028864 | bytes 74448896 | tf_op jit(solution)/shard_map/egcf,efd->egcd/dot_general | solution.py:81
  569.2 18.7 %copy.53 = bf16[2,256,16,1024]{3,2,0,1:T(8,128)(2,1)} copy(bf16[2,256,16,1024]{3,1,2,0:T(8,128)(2,1)} %convolution_convert_fusion) | data formatting | bytes 33554432 | tf_op jit(solution)/shard_map/convert_element_type | solution.py:81
  587.9 13.6 %all-to-all-start.1 = ((bf16[2,256,16,1024]{3,2,0,1:T(8,128)(2,1)}), bf16[2,256,16,1024]{3,2,0,1:T(8,128)(2,1)}, u32[]{:S(2)}, u32[]{:S(2)}) async-start(bf16[2,256,16,1024]{3,2,0,1:T(8,128)(2,1)} %copy.53), calls=%async_computation.1 | async-start | bytes 33554432 | tf_op jit(solution)/shard_map/all_to_all | solution.py:82
  601.6 0.6 multiply_reduce_fusion
  602.2 230.8 %psum.7 = f32[]{:T(128)} all-reduce(f32[]{:T(128)} %multiply_reduce_fusion), channel_id=1, replica_groups=mesh['ep'=16] {'ep'}, use_global_device_ids=true, to_apply=%region_17.18 | all-reduce | flops 1 | bytes 8 | tf_op jit(solution)/shard_map/psum | solution.py:85
  833.7 0.0 all-to-all-done.1
  833.7 31.1 %copy.78 = bf16[2,16,16,16,1024]{4,0,1,3,2:T(2,128)(2,1)} copy(bf16[2,16,16,16,1024]{4,3,0,2,1:T(8,128)(2,1)} %bitcast.27) | data formatting | bytes 33554432 | tf_op jit(solution)/shard_map/all_to_all | solution.py:82
  864.8 25.0 %all_to_all.33 = bf16[32,16,16,1024]{3,0,2,1:T(8,128)(2,1)} reshape(bf16[16,2,16,16,1024]{4,1,0,3,2:T(2,128)(2,1)} %bitcast.143) | data formatting | bytes 33554432 | tf_op jit(solution)/shard_map/all_to_all | solution.py:82
  889.8 0.0 copy-start.1
  889.8 16.8 %fusion.15 = bf16[16,256,1024]{2,1,0:T(8,128)(2,1)} fusion(bf16[16,256,1024]{2,1,0:T(8,128)(2,1)} %copy-done.28, bf16[32,16,16,1024]{3,0,2,1:T(8,128)(2,1)} %all_to_all.33, f32[16,256]{1,0:T(8,128)S(1)} %copy-done.23, f32[16,256]{1,0:T(8,128)S(1)} %add_divide_fusion.1, pred[16,256,16]{1,2,0:T(8,128)(4,1)S(1)} %copy-done.12, ...), kind=kOutput, calls=%fused_computation.25 | convolution fusion | flops 4320133120 | bytes 33980416 | tf_op jit(solution)/shard_map/gsec,egcd->gsd/dot_general | solution.py:83
  (64 shorter events, 0.2 us)
Async XLA Ops:
  0.6 20.8 %copy-start = (bf16[1024,16,64]{0,2,1:T(8,128)(2,1)S(1)}, bf16[1024,16,64]{0,2,1:T(8,128)(2,1)}, u32[]{:S(2)}) copy-start(bf16[1024,16,64]{0,2,1:T(8,128)(2,1)} %param.19) | copy-start | bytes 6291460
  6.6 46.3 %copy-start.18 = (pred[16,256]{1,0:T(8,128)(4,1)}, pred[16,256]{1,0:T(8,128)(4,1)S(1)}, u32[]{:S(2)}) copy-start(pred[16,256]{1,0:T(8,128)(4,1)S(1)} %broadcast_compare_fusion) | copy-start | bytes 12292
  7.2 14.2 %copy-start.2 = (f32[1024]{0:T(1024)S(1)}, f32[1024]{0:T(1024)}, u32[]{:S(2)}) copy-start(f32[1024]{0:T(1024)} %param.17) | copy-start | bytes 12292
  53.0 68.7 %copy-start.25 = (bf16[1024,16,64]{0,2,1:T(8,128)(2,1)S(1)}, bf16[1024,16,64]{0,2,1:T(8,128)(2,1)}, u32[]{:S(2)}) copy-start(bf16[1024,16,64]{0,2,1:T(8,128)(2,1)} %param.20) | copy-start | bytes 6291460
  164.3 15.8 %copy-start.21 = (s32[16,256,2]{1,2,0:T(2,128)S(1)}, s32[16,256,2]{1,2,0:T(2,128)}, u32[]{:S(2)}) copy-start(s32[16,256,2]{1,2,0:T(2,128)} %param.16) | copy-start | bytes 98308
  164.3 19.1 %copy-start.26 = (f32[1024,32]{0,1:T(8,128)S(1)}, f32[1024,32]{0,1:T(8,128)}, u32[]{:S(2)}) copy-start(f32[1024,32]{0,1:T(8,128)} %param.23) | copy-start | bytes 393220
  164.3 19.1 %copy-start.27 = (f32[1024]{0:T(1024)S(1)}, f32[1024]{0:T(1024)}, u32[]{:S(2)}) copy-start(f32[1024]{0:T(1024)} %param.22) | copy-start | bytes 12292
  180.0 3.4 copy-start.28
  180.0 10.8 %copy-start.19 = (pred[16,256]{1,0:T(8,128)(4,1)S(1)}, pred[16,256]{1,0:T(8,128)(4,1)}, u32[]{:S(2)}) copy-start(pred[16,256]{1,0:T(8,128)(4,1)} %copy-done.18) | copy-start | bytes 12292
  180.0 11.9 %copy-start.20 = (pred[16,2,128]{2,1,0:T(4,128)(4,1)S(1)}, pred[16,2,128]{2,1,0:T(4,128)(4,1)}, u32[]{:S(2)}) copy-start(pred[16,2,128]{2,1,0:T(4,128)(4,1)} %and.94) | copy-start | bytes 12292
  180.2 33.2 %copy-start.3 = (pred[16,256,32]{1,2,0:T(8,128)(4,1)}, pred[16,256,32]{1,2,0:T(8,128)(4,1)S(1)}, u32[]{:S(2)}) copy-start(pred[16,256,32]{1,2,0:T(8,128)(4,1)S(1)} %iota_compare_fusion.1) | copy-start | bytes 393220
  180.2 33.1 %copy-start.5 = (pred[16,256,32]{1,2,0:T(8,128)(4,1)}, pred[16,256,32]{1,2,0:T(8,128)(4,1)S(1)}, u32[]{:S(2)}) copy-start(pred[16,256,32]{1,2,0:T(8,128)(4,1)S(1)} %iota_compare_fusion.3) | copy-start | bytes 393220
  183.4 18.9 %copy-start.17 = (s32[16,256]{1,0:T(8,128)S(1)}, s32[16,256]{1,0:T(8,128)}, u32[]{:S(2)}) copy-start(s32[16,256]{1,0:T(8,128)} %param.14) | copy-start | bytes 49156
  183.4 18.9 %copy-start.22 = (f32[16,256]{1,0:T(8,128)S(1)}, f32[16,256]{1,0:T(8,128)}, u32[]{:S(2)}) copy-start(f32[16,256]{1,0:T(8,128)} %param.15) | copy-start | bytes 49156
  191.9 11.1 %copy-start.13 = (f32[16,256]{1,0:T(8,128)}, f32[16,256]{1,0:T(8,128)S(1)}, u32[]{:S(2)}) copy-start(f32[16,256]{1,0:T(8,128)S(1)} %get-tuple-element.3) | copy-start | bytes 49156
  191.9 11.1 %copy-start.15 = (f32[16,256]{1,0:T(8,128)}, f32[16,256]{1,0:T(8,128)S(1)}, u32[]{:S(2)}) copy-start(f32[16,256]{1,0:T(8,128)S(1)} %get-tuple-element.4) | copy-start | bytes 49156
  202.3 21.8 %copy-start.7 = (s32[16,32]{1,0:T(8,128)}, s32[16,32]{1,0:T(8,128)S(1)}, u32[]{:S(2)}) copy-start(s32[16,32]{1,0:T(8,128)S(1)} %get-tuple-element.6) | copy-start | bytes 6148
  203.0 21.1 %copy-start.9 = (pred[16,256,16]{1,2,0:T(8,128)(4,1)}, pred[16,256,16]{1,2,0:T(8,128)(4,1)S(1)}, u32[]{:S(2)}) copy-start(pred[16,256,16]{1,2,0:T(8,128)(4,1)S(1)} %fusion.76) | copy-start | bytes 196612
  213.3 10.7 %copy-start.11 = (pred[16,256,16]{1,2,0:T(8,128)(4,1)}, pred[16,256,16]{1,2,0:T(8,128)(4,1)S(1)}, u32[]{:S(2)}) copy-start(pred[16,256,16]{1,2,0:T(8,128)(4,1)S(1)} %fusion.77) | copy-start | bytes 196612
  587.9 13.7 %copy-start.8 = (s32[16,32]{1,0:T(8,128)S(1)}, s32[16,32]{1,0:T(8,128)}, u32[]{:S(2)}) copy-start(s32[16,32]{1,0:T(8,128)} %copy-done.7) | copy-start | bytes 6148
  587.9 13.7 %copy-start.24 = (f32[16,32]{1,0:T(8,128)S(1)}, f32[16,32]{1,0:T(8,128)}, u32[]{:S(2)}) copy-start(f32[16,32]{1,0:T(8,128)} %get-tuple-element.2) | copy-start | bytes 6148
  587.9 245.7 %copy-start.14 = (f32[16,256]{1,0:T(8,128)S(1)}, f32[16,256]{1,0:T(8,128)}, u32[]{:S(2)}) copy-start(f32[16,256]{1,0:T(8,128)} %copy-done.13) | copy-start | bytes 49156
  587.9 245.7 %copy-start.16 = (f32[16,256]{1,0:T(8,128)S(1)}, f32[16,256]{1,0:T(8,128)}, u32[]{:S(2)}) copy-start(f32[16,256]{1,0:T(8,128)} %copy-done.15) | copy-start | bytes 49156
  587.9 245.8 %all-to-all-start.1 = ((bf16[2,256,16,1024]{3,2,0,1:T(8,128)(2,1)}), bf16[2,256,16,1024]{3,2,0,1:T(8,128)(2,1)}, u32[]{:S(2)}, u32[]{:S(2)}) async-start(bf16[2,256,16,1024]{3,2,0,1:T(8,128)(2,1)} %copy.53), calls=%async_computation.1 | async-start | bytes 33554432 | tf_op jit(solution)/shard_map/all_to_all | solution.py:82
  864.7 25.0 %copy-start.4 = (pred[16,256,32]{1,2,0:T(8,128)(4,1)S(1)}, pred[16,256,32]{1,2,0:T(8,128)(4,1)}, u32[]{:S(2)}) copy-start(pred[16,256,32]{1,2,0:T(8,128)(4,1)} %copy-done.3) | copy-start | bytes 393220
  864.7 25.0 %copy-start.6 = (pred[16,256,32]{1,2,0:T(8,128)(4,1)S(1)}, pred[16,256,32]{1,2,0:T(8,128)(4,1)}, u32[]{:S(2)}) copy-start(pred[16,256,32]{1,2,0:T(8,128)(4,1)} %copy-done.5) | copy-start | bytes 393220
  864.7 25.0 %copy-start.10 = (pred[16,256,16]{1,2,0:T(8,128)(4,1)S(1)}, pred[16,256,16]{1,2,0:T(8,128)(4,1)}, u32[]{:S(2)}) copy-start(pred[16,256,16]{1,2,0:T(8,128)(4,1)} %copy-done.9) | copy-start | bytes 196612
  864.8 25.0 %copy-start.12 = (pred[16,256,16]{1,2,0:T(8,128)(4,1)S(1)}, pred[16,256,16]{1,2,0:T(8,128)(4,1)}, u32[]{:S(2)}) copy-start(pred[16,256,16]{1,2,0:T(8,128)(4,1)} %copy-done.11) | copy-start | bytes 196612
  864.8 25.0 %copy-start.23 = (f32[16,256]{1,0:T(8,128)S(1)}, f32[16,256]{1,0:T(8,128)}, u32[]{:S(2)}) copy-start(f32[16,256]{1,0:T(8,128)} %get-tuple-element.8) | copy-start | bytes 49156
  889.8 16.8 %copy-start.1 = (bf16[1024,16,64]{0,2,1:T(8,128)(2,1)S(1)}, bf16[1024,16,64]{0,2,1:T(8,128)(2,1)}, u32[]{:S(2)}) copy-start(bf16[1024,16,64]{0,2,1:T(8,128)(2,1)} %param.19) | copy-start | bytes 6291460
where the time goes:
time: 918 us; the launch traced here: 908 us
  blocking collectives  425 us (46%)
  matrix products  268 us (29%)
  local copies, waits for them, and re-layouts  102 us (11%)
  other arithmetic  96.8 us (11%)
  starting transfers between devices  13.6 us (1%)
    psum x1, blocking collectives, local_step(): aux_loss = lax.psum(aux_sum, 'ep') * experts / (groups_local * n_dev)  231 us
    all_to_all x1, blocking collectives, local_step(): received = lax.all_to_all(send_buf, 'ep', 0, 1, tiled=True)  194 us
    dot_general x1, matrix products, local_step(): jnp.einsum('egcd,edf->egcf', received, w_in, preferred_element_type=jnp.f...  72.1 us
    sub x1, other arithmetic, attention_block(): attn_probs = jax.nn.softmax(scores, axis=-1).astype(jnp.bfloat16)  68.7 us
    dot_general x1, matrix products, local_step(): jnp.einsum('egcf,efd->egcd', inner_act, w_out, preferred_element_type=jnp...  56.8 us
    all_to_all x2, local copies, waits for them, and re-layouts, local_step(): returned = lax.all_to_all(expert_out, 'ep', 1, 0, tiled=True)  56.1 us
    dot_general x1, matrix products, attention_block(): jnp.einsum('gqhc,gkhc->ghqk', q_heads, k_heads, preferred_element_type=jn...  31.6 us
    dot_general x1, matrix products, attention_block(): jnp.einsum('ghqk,gkhc->gqhc', attn_probs, v_heads, preferred_element_type...  27.7 us
  transfers between devices with their start and end apart: 1, of which 0 were waited for; matrix products, arithmetic and copies ran while one was open for 0% of the time, Pallas kernels for 0%

commit v1 on v0

v1 whole, which is shorter than its diff:
```python
import functools
import jax
import jax.numpy as jnp
from jax import lax
from jax.experimental import pallas as pl
from jax.experimental.pallas import tpu as pltpu
from jax.sharding import PartitionSpec as P

NORM_EPS = 1e-6
MESH = pl.DeviceIdType.MESH
F32 = jnp.float32
BF16 = jnp.bfloat16
LOG2E = 1.4426950408889634


def norm_rows(x, scale):
    inv = lax.rsqrt(jnp.mean(x * x, axis=-1, keepdims=True) + NORM_EPS)
    return (x * inv * scale).astype(BF16)


def dot_nt(a, b):
    return lax.dot_general(a, b, (((1,), (1,)), ((), ())), preferred_element_type=F32)


def dot_tn(a, b):
    return lax.dot_general(a, b, (((0,), (0,)), ((), ())), preferred_element_type=F32)


def peer_order(n):
    full = [2, 4, 8, 3, 5, 9, 6, 12, 10, 7, 13, 11, 14, 15, 1]
    return [k for k in full if k < n] if n == 16 else list(range(1, n))


def attend_kernel(n, heads, cap, groups, meta_ref, tok_ref, na_ref, wqkv_ref, wo_ref, nm_ref, wg_ref,
                  h_ref, aux_ref, loss_ref, recv_ref,
                  qkv_ref, ctx_ref, xs_ref, send_sem, recv_sem, own_sem):
    me = lax.axis_index("ep")
    g = pl.program_id(0)
    seq, d = tok_ref.shape[1], tok_ref.shape[2]
    experts = wg_ref.shape[0] // 3
    rows = experts * cap // n
    ks = peer_order(n)

    @pl.when(g == 0)
    def _():
        barrier = pltpu.get_barrier_semaphore()
        for k in ks:
            pl.semaphore_signal(barrier, inc=1, device_id=(me ^ k,), device_id_type=MESH)
        pl.semaphore_wait(barrier, n - 1)
        loss_ref[...] = jnp.zeros_like(loss_ref)

    @pl.when(g > 0)
    def _():
        p = g - 1
        for k in ks:
            peer = me ^ k
            pltpu.make_async_remote_copy(
                src_ref=xs_ref.at[p, pl.ds(pl.multiple_of(peer * rows, rows), rows)],
                dst_ref=recv_ref.at[me, p],
                send_sem=send_sem.at[p], recv_sem=recv_sem.at[me],
                device_id=(peer,), device_id_type=MESH).start()
        pltpu.make_async_copy(xs_ref.at[p, pl.ds(pl.multiple_of(me * rows, rows), rows)],
                              recv_ref.at[me, p], own_sem).start()

    @pl.when(g < groups)
    def _():
        a = norm_rows(tok_ref[0].astype(F32), na_ref[...])
        for c in range(3):
            qkv_ref[:, c * d:(c + 1) * d] = jnp.dot(
                a, wqkv_ref[:, c * d:(c + 1) * d], preferred_element_type=F32).astype(BF16)
        key_ok = meta_ref[0, 2:3, :] == 1.0
        low = lax.broadcasted_iota(jnp.int32, (seq, 128), 1) < 64
        factor = 0.125 * LOG2E

        def probs(q, k):
            s = jnp.where(key_ok, dot_nt(q, k), -1e30)
            e = jnp.exp2((s - jnp.max(s, axis=-1, keepdims=True)) * factor)
            return (e * (1.0 / jnp.sum(e, axis=-1, keepdims=True))).astype(BF16)

        def pair(i, carry):
            off = pl.multiple_of(i * 128, 128)
            q = qkv_ref[:, pl.ds(off, 128)]
            k = qkv_ref[:, pl.ds(pl.multiple_of(d + off, 128), 128)]
            v = qkv_ref[:, pl.ds(pl.multiple_of(2 * d + off, 128), 128)]
            zero = jnp.zeros_like(q)
            p0 = probs(jnp.where(low, q, zero), k)
            p1 = probs(jnp.where(low, zero, q), k)
            c = jnp.dot(p0, jnp.where(low, v, zero), preferred_element_type=F32)
            c += jnp.dot(p1, jnp.where(low, zero, v), preferred_element_type=F32)
            ctx_ref[:, pl.ds(off, 128)] = c.astype(BF16)
            return carry

        lax.fori_loop(0, heads // 2, pair, 0, unroll=2)
        attn = jnp.dot(ctx_ref[...], wo_ref[...], preferred_element_type=F32)
        h = (tok_ref[0].astype(F32) + attn).astype(BF16)
        h_ref[0] = h
        b = norm_rows(h.astype(F32), nm_ref[...])

        lg = dot_nt(wg_ref[...], b)
        lg = lg[:experts] + (lg[experts:2 * experts] + lg[2 * experts:])
        ex = jnp.exp(lg - jnp.max(lg, axis=0, keepdims=True))
        p = ex / jnp.sum(ex, axis=0, keepdims=True)
        c1 = meta_ref[0, 0:1, :]
        c2 = meta_ref[0, 1:2, :]
        draw = meta_ref[0, 3:4, :]
        valid = jnp.where(meta_ref[0, 2:3, :] == 1.0, 1.0, 0.0)
        ids = lax.broadcasted_iota(jnp.int32, (experts, seq), 0).astype(F32)
        hot1 = jnp.where(ids == c1, 1.0, 0.0)
        hot2 = jnp.where(ids == c2, 1.0, 0.0)
        p1 = jnp.sum(hot1 * p, axis=0, keepdims=True)
        p2 = jnp.sum(hot2 * p, axis=0, keepdims=True)
        g1 = p1 / (p1 + p2)
        g2 = p2 / (p1 + p2)
        want2 = valid * jnp.where(draw < 2.0 * g2, 1.0, 0.0)
        take1 = hot1 * valid
        take2 = hot2 * want2
        upper = jnp.where(lax.broadcasted_iota(jnp.int32, (seq, seq), 0)
                          <= lax.broadcasted_iota(jnp.int32, (seq, seq), 1), 1.0, 0.0).astype(BF16)
        cum1 = jnp.dot(take1.astype(BF16), upper, preferred_element_type=F32)
        cum2 = jnp.dot(take2.astype(BF16), upper, preferred_element_type=F32)
        count1 = jnp.sum(take1, axis=1, keepdims=True)
        pos1 = jnp.sum((cum1 - 1.0) * take1, axis=0, keepdims=True)
        pos2 = jnp.sum((cum2 - 1.0 + jnp.minimum(count1, float(cap))) * take2, axis=0, keepdims=True)
        slot1 = jnp.where((valid > 0.5) & (pos1 < float(cap)), c1 * float(cap) + pos1, -1.0)
        slot2 = jnp.where((want2 > 0.5) & (pos2 < float(cap)), c2 * float(cap) + pos2, -1.0)
        half = experts * cap // 2
        for part in range(2):
            slots = lax.broadcasted_iota(jnp.int32, (half, seq), 0).astype(F32) + float(part * half)
            pick = jnp.where((slots == slot1) | (slots == slot2), 1.0, 0.0).astype(BF16)
            xs_ref[g, part * half:(part + 1) * half, :] = jnp.dot(
                pick, b, preferred_element_type=F32).astype(BF16)
        density = jnp.sum(p * valid, axis=1, keepdims=True) * (1.0 / seq)
        part_loss = jnp.sum(count1 * (1.0 / seq) * density, axis=0, keepdims=True)
        loss_ref[...] += part_loss
        aux_ref[0] = jnp.concatenate([slot1, slot2, g1, g2, g1, g1, g1, g1], axis=0)

    @pl.when(g == groups)
    def _():
        for i in range(groups):
            block = xs_ref.at[i, pl.ds(0, (n - 1) * rows)]
            pltpu.make_async_copy(block, block, send_sem.at[i]).wait()
        for k in ks:
            block = recv_ref.at[me ^ k]
            pltpu.make_async_copy(block, block, recv_sem.at[me ^ k]).wait()
        block = recv_ref.at[me]
        pltpu.make_async_copy(block, block, own_sem).wait()


def expert_kernel(n, cap, groups, slots, aux_ref, x_ref, h_ref, loss_in, w_in_hbm, w_out_hbm,
                  out_ref, loss_ref,
                  w_in, w_out, mid_ref, z_ref, ret_ref, lbuf, w_sem, send_sem, recv_sem, lsend_sem, lrecv_sem):
    me = lax.axis_index("ep")
    r = pl.program_id(0)
    e_loc, d, ff = w_in.shape
    rows = e_loc * cap
    seq = h_ref.shape[1]
    ks = peer_order(n)

    def weight_copy(e, which):
        if which == 0:
            return pltpu.make_async_copy(w_in_hbm.at[e], w_in.at[e], w_sem.at[e, 0])
        return pltpu.make_async_copy(w_out_hbm.at[e], w_out.at[e], w_sem.at[e, 1])

    @pl.when(r == 0)
    def _():
        for e in range(e_loc):
            weight_copy(e, 0).start()
            weight_copy(e, 1).start()
        barrier = pltpu.get_barrier_semaphore()
        for k in ks:
            pl.semaphore_signal(barrier, inc=1, device_id=(me ^ k,), device_id_type=MESH)
        pl.semaphore_wait(barrier, n - 1)
        for k in ks:
            pltpu.make_async_remote_copy(
                src_ref=loss_in, dst_ref=lbuf.at[me], send_sem=lsend_sem, recv_sem=lrecv_sem,
                device_id=(me ^ k,), device_id_type=MESH).start()
        lbuf[me] = loss_in[...]

    @pl.when((r > 0) & (r <= groups))
    def _():
        p = r - 1
        for k in ks:
            peer = me ^ k
            pltpu.make_async_remote_copy(
                src_ref=z_ref.at[lax.rem(p, slots), peer],
                dst_ref=ret_ref.at[p, pl.ds(pl.multiple_of(me * rows, rows), rows)],
                send_sem=send_sem.at[lax.rem(p, slots)], recv_sem=recv_sem.at[p],
                device_id=(peer,), device_id_type=MESH).start()
        ret_ref[p, pl.ds(pl.multiple_of(me * rows, rows), rows), :] = z_ref[lax.rem(p, slots), me]

    def wait_sends(s):
        block = z_ref.at[s, pl.ds(0, n - 1)]
        pltpu.make_async_copy(block, block, send_sem.at[s]).wait()

    @pl.when(r < groups)
    def _():
        s = lax.rem(r, slots)

        @pl.when(r >= slots)
        def _():
            wait_sends(s)

        for e in range(e_loc):
            @pl.when(r == 0)
            def _():
                weight_copy(e, 0).wait()
            lhs = x_ref[:, 0, e * cap:(e + 1) * cap, :].reshape(n * cap, d)
            for c in range(2):
                cols = slice(c * (ff // 2), (c + 1) * (ff // 2))
                up = jnp.dot(lhs, w_in[e, :, cols], preferred_element_type=F32)
                mid_ref[:, cols] = jnp.maximum(up, 0.0).astype(BF16)

            @pl.when(r == 0)
            def _():
                weight_copy(e, 1).wait()
            for c in range(2):
                cols = slice(c * (d // 2), (c + 1) * (d // 2))
                down = jnp.dot(mid_ref[...], w_out[e, :, cols], preferred_element_type=F32)
                z_ref[s, :, e * cap:(e + 1) * cap, cols] = down.astype(BF16).reshape(n, cap, d // 2)

    @pl.when(r >= groups)
    def _():
        g = r - groups
        block = ret_ref.at[g, pl.ds(0, (n - 1) * rows)]
        pltpu.make_async_copy(block, block, recv_sem.at[g]).wait()
        slot1 = aux_ref[0, 0:1, :]
        slot2 = aux_ref[0, 1:2, :]
        g1 = aux_ref[0, 2:3, :]
        g2 = aux_ref[0, 3:4, :]
        ids = lax.broadcasted_iota(jnp.int32, (n * rows, seq), 0).astype(F32)
        comb = (jnp.where(ids == slot1, g1, 0.0) + jnp.where(ids == slot2, g2, 0.0)).astype(BF16)
        out_ref[0] = (h_ref[0].astype(F32) + dot_tn(comb, ret_ref[g])).astype(BF16)

    @pl.when(r == 2 * groups - 1)
    def _():
        for s in range(slots):
            wait_sends(s)
        pltpu.make_async_copy(lbuf.at[pl.ds(0, n - 1)], lbuf.at[pl.ds(0, n - 1)], lsend_sem).wait()
        pltpu.make_async_copy(lbuf.at[pl.ds(0, n - 1)], lbuf.at[pl.ds(0, n - 1)], lrecv_sem).wait()
        loss_ref[...] = jnp.sum(lbuf[...], axis=0)


def solution(mesh):
    n = mesh.shape["ep"]

    def local_step(tokens, pad_mask, second_draw, choices, norm_attn, w_query, w_key, w_value, w_attn_out, norm_moe, w_gate, w_in, w_out):
        groups, seq, d = tokens.shape
        heads = w_query.shape[1]
        experts = w_gate.shape[1]
        e_loc, _, ff = w_in.shape
        cap = (2 * seq + experts - 1) // experts
        rows = e_loc * cap
        flat = [w.reshape(d, d) for w in (w_query, w_key, w_value)]
        wqkv = jnp.concatenate(flat, axis=1)
        wo = w_attn_out.reshape(d, d)
        g_hi = lax.reduce_precision(w_gate, 8, 7)
        g_mid = lax.reduce_precision(w_gate - g_hi, 8, 7)
        g_lo = w_gate - g_hi - g_mid
        wg = jnp.concatenate([g_hi, g_mid, g_lo], axis=1).astype(BF16).T
        meta = jnp.stack([choices[:, :, 0].astype(F32), choices[:, :, 1].astype(F32),
                          pad_mask.astype(F32), second_draw] + [second_draw] * 4, axis=1)
        const = dict(pipeline_mode=pl.Buffered(1))
        last = groups - 1
        hidden, aux, loss, recv = pl.pallas_call(
            functools.partial(attend_kernel, n, heads, cap, groups),
            grid=(groups + 1,),
            out_shape=(jax.ShapeDtypeStruct((groups, seq, d), BF16),
                       jax.ShapeDtypeStruct((groups, 8, seq), F32),
                       jax.ShapeDtypeStruct((8, 128), F32),
                       jax.ShapeDtypeStruct((n, groups, rows, d), BF16)),
            in_specs=[pl.BlockSpec((1, 8, seq), lambda g: (jnp.minimum(g, last), 0, 0)),
                      pl.BlockSpec((1, seq, d), lambda g: (jnp.minimum(g, last), 0, 0)),
                      pl.BlockSpec((1, d), lambda g: (0, 0), **const),
                      pl.BlockSpec((d, 3 * d), lambda g: (0, 0), **const),
                      pl.BlockSpec((d, d), lambda g: (0, 0), **const),
                      pl.BlockSpec((1, d), lambda g: (0, 0), **const),
                      pl.BlockSpec((3 * experts, d), lambda g: (0, 0), **const)],
            out_specs=(pl.BlockSpec((1, seq, d), lambda g: (jnp.minimum(g, last), 0, 0)),
                       pl.BlockSpec((1, 8, seq), lambda g: (jnp.minimum(g, last), 0, 0)),
                       pl.BlockSpec((8, 128), lambda g: (0, 0)),
                       pl.BlockSpec(memory_space=pl.ANY)),
            scratch_shapes=[pltpu.VMEM((seq, 3 * d), BF16), pltpu.VMEM((seq, d), BF16),
                            pltpu.VMEM((groups, n * rows, d), BF16),
                            pltpu.SemaphoreType.DMA((groups,)), pltpu.SemaphoreType.DMA((n,)),
                            pltpu.SemaphoreType.DMA],
            compiler_params=pltpu.CompilerParams(collective_id=0, has_side_effects=True,
                                                 vmem_limit_bytes=60 * 2**20),
        )(meta, tokens, norm_attn.reshape(1, d), wqkv, wo, norm_moe.reshape(1, d), wg)

        slots = 6
        out, loss = pl.pallas_call(
            functools.partial(expert_kernel, n, cap, groups, slots),
            grid=(2 * groups,),
            out_shape=(jax.ShapeDtypeStruct((groups, seq, d), BF16), jax.ShapeDtypeStruct((8, 128), F32)),
            in_specs=[pl.BlockSpec((1, 8, seq), lambda r: (jnp.maximum(r - groups, 0), 0, 0)),
                      pl.BlockSpec((n, 1, rows, d), lambda r: (0, jnp.minimum(r, last), 0, 0)),
                      pl.BlockSpec((1, seq, d), lambda r: (jnp.maximum(r - groups, 0), 0, 0)),
                      pl.BlockSpec((8, 128), lambda r: (0, 0), **const),
                      pl.BlockSpec(memory_space=pl.ANY),
                      pl.BlockSpec(memory_space=pl.ANY)],
            out_specs=(pl.BlockSpec((1, seq, d), lambda r: (jnp.maximum(r - groups, 0), 0, 0)),
                       pl.BlockSpec((8, 128), lambda r: (0, 0))),
            scratch_shapes=[pltpu.VMEM((e_loc, d, ff), BF16), pltpu.VMEM((e_loc, ff, d), BF16),
                            pltpu.VMEM((n * cap, ff), BF16), pltpu.VMEM((slots, n, rows, d), BF16),
                            pltpu.VMEM((groups, n * rows, d), BF16), pltpu.VMEM((n, 8, 128), F32),
                            pltpu.SemaphoreType.DMA((e_loc, 2)), pltpu.SemaphoreType.DMA((slots,)),
                            pltpu.SemaphoreType.DMA((groups,)), pltpu.SemaphoreType.DMA, pltpu.SemaphoreType.DMA],
            compiler_params=pltpu.CompilerParams(collective_id=1, has_side_effects=True,
                                                 vmem_limit_bytes=63 * 2**20),
        )(aux, recv, hidden, loss, w_in, w_out)
        aux_loss = loss[0, 0] * experts / (groups * n)
        return out, aux_loss

    by_group = P("ep")
    replicated = P()
    in_specs = (by_group, by_group, by_group, by_group, replicated, replicated, replicated, replicated, replicated, replicated, replicated, by_group, by_group)
    return jax.shard_map(local_step, mesh=mesh, in_specs=in_specs, out_specs=(by_group, replicated), check_vma=False)
```

time: 918 us -> 437 us (0.48)
  blocking collectives: 425 us -> 0 us
  Pallas kernels: 0 us -> 404 us
  matrix products: 268 us -> 0 us
  other arithmetic: 96.8 us -> 8.57 us
  local copies, waits for them, and re-layouts: 102 us -> 21.6 us
  starting transfers between devices: 13.6 us -> 0 us
    pallas_call x0 -> x2, Pallas kernels: none -> 404 us  [the longest x1 203 us: local_step(): pl.pallas_call(functools.partial(expert_kernel, n, cap, groups, slots), g...]
    dot_general x10 -> x0, matrix products: 268 us -> none  [the longest x1 72.1 us: local_step(): jnp.einsum('egcd,edf->egcf', received, w_in, preferred_element_type=jnp.f...]
    psum x1 -> x0, blocking collectives: 231 us -> none  [local_step(): aux_loss = lax.psum(aux_sum, 'ep') * experts / (groups_local * n_dev)]
    all_to_all x1 -> x0, blocking collectives: 194 us -> none  [local_step(): received = lax.all_to_all(send_buf, 'ep', 0, 1, tiled=True)]
    sub x1 -> x0, other arithmetic: 68.7 us -> none  [attention_block(): attn_probs = jax.nn.softmax(scores, axis=-1).astype(jnp.bfloat16)]
    all_to_all x3 -> x0, local copies, waits for them, and re-layouts: 62.7 us -> none  [the longest x2 56.1 us: local_step(): returned = lax.all_to_all(expert_out, 'ep', 1, 0, tiled=True)]
    convert_element_type x2 -> x0, local copies, waits for them, and re-layouts: 34.1 us -> none  [the longest x1 18.7 us: local_step(): jnp.einsum('egcf,efd->egcd', inner_act, w_out, preferred_element_type=jnp...]
    another operation x4 -> x1, other arithmetic: 18.6 us -> 0.93 us
  transfers between devices with their start and end apart: 1 -> 0, of which waited for: 0 -> 0; matrix products, arithmetic and copies ran while one was open for 0% -> 0% of each run, Pallas kernels for 0% -> 0%
where the time goes in v1:
time: 437 us; the launch traced here: 436 us
  Pallas kernels  404 us (92%)
  local copies, waits for them, and re-layouts  21.6 us (5%)
  other arithmetic  8.57 us (2%)
    pallas_call x1, Pallas kernels, local_step(): pl.pallas_call(functools.partial(expert_kernel, n, cap, groups, slots), g...  203 us
    pallas_call x1, Pallas kernels, local_step(): pl.pallas_call(functools.partial(attend_kernel, n, heads, cap, groups), g...  201 us
    reshape x3, local copies, waits for them, and re-layouts, local_step(): flat = [w.reshape(d, d) for w in (w_query, w_key, w_value)]  10.7 us

profile of v1, /device:TPU:0, one launch (start us, length us, event | category | flops | bytes accessed | tf_op | source)
XLA Modules:
  0.0 436.3 jit_solution(8944696998093663305)
XLA Ops:
  0.6 0.7 convert_element_type.34
  1.4 0.7 stack.7
  2.1 0.9 convert_bitcast_fusion
  3.0 0.8 stack.8.meta_ref
  3.8 0.9 reduce-precision_convert_fusion.1
  4.7 0.7 maximum_bitcast_fusion.wg_ref
  5.4 2.9 copy.18
  8.3 3.9 copy.19
  12.2 3.9 copy.20
  16.2 5.4 %pad_maximum_fusion.wqkv_ref = bf16[1024,3072]{1,0:T(8,128)(2,1)} fusion(bf16[1024,1024]{1,0:T(8,128)(2,1)} %copy.20, bf16[1024,1024]{1,0:T(8,128)(2,1)} %copy.19, bf16[1024,1024]{1,0:T(8,128)(2,1)S(1)} %copy.18), kind=kLoop, calls=%fused_computation | loop fusion | flops 18874368 | bytes 12582912 | tf_op jit(solution)/shard_map/concatenate | solution.py:254
  21.5 201.2 %shard_map.140 = (bf16[16,256,1024]{2,1,0:T(8,128)(2,1)}, f32[16,8,256]{2,1,0:T(8,128)}, f32[8,128]{1,0:T(8,128)}, bf16[16,16,32,1024]{3,2,1,0:T(8,128)(2,1)}) custom-call(f32[16,8,256]{2,1,0:T(8,128)} %stack.8.meta_ref, bf16[16,256,1024]{2,1,0:T(8,128)(2,1)} %tok_ref.1, f32[1,1024]{1,0:T(1,128)} %bitcast.17, bf16[1024,3072]{1,0:T(8,128)(2,1)} %pad_maximum_fusion.wqkv_ref, ...), custom_call_target="tpu_custom_call" | custom-call | tf_op jit(solution)/shard_map/pallas_call | solution.py:264
  222.7 202.5 %shard_map.141 = (bf16[16,256,1024]{2,1,0:T(8,128)(2,1)}, f32[8,128]{1,0:T(8,128)}) custom-call(f32[16,8,256]{2,1,0:T(8,128)} %get-tuple-element.8.aux_ref, bf16[16,16,32,1024]{3,2,1,0:T(8,128)(2,1)} %get-tuple-element.9.x_ref, bf16[16,256,1024]{2,1,0:T(8,128)(2,1)} %get-tuple-element.10.h_ref, f32[8,128]{1,0:T(8,128)} %get-tuple-element.11.loss_in, ...), custom_call_target="tpu_custom_call" | custom-call | tf_op jit(solution)/shard_map/pallas_call | solution.py:291
  425.2 1.2 slice.11
  427.1 8.1 %copy.22 = bf16[16,256,1024]{2,1,0:T(8,128)(2,1)} copy(bf16[16,256,1024]{2,1,0:T(8,128)(2,1)} %get-tuple-element.21) | data formatting | bytes 16777216
  (1 shorter events, 0.0 us)

commit v2 on v0

v2 whole, which is shorter than its diff:
```python
import functools
import jax
import jax.numpy as jnp
from jax import lax
from jax.experimental import pallas as pl
from jax.experimental.pallas import tpu as pltpu
from jax.sharding import PartitionSpec as P

NORM_EPS = 1e-6
MESH = pl.DeviceIdType.MESH
F32 = jnp.float32
BF16 = jnp.bfloat16
LOG2E = 1.4426950408889634


def norm_rows(x, scale):
    inv = lax.rsqrt(jnp.mean(x * x, axis=-1, keepdims=True) + NORM_EPS)
    return (x * inv * scale).astype(BF16)


def dot_nn(a, b):
    return jnp.dot(a, b, preferred_element_type=F32)


def dot_nt(a, b):
    return lax.dot_general(a, b, (((1,), (1,)), ((), ())), preferred_element_type=F32)


def dot_tn(a, b):
    return lax.dot_general(a, b, (((0,), (0,)), ((), ())), preferred_element_type=F32)


def peer_order(n):
    full = [2, 4, 8, 3, 5, 9, 6, 12, 10, 7, 13, 11, 14, 15, 1]
    return full if n == 16 else list(range(1, n))


def layer_kernel(n, heads, cap, groups, mask_ref, draw_ref, pick_ref, tok_ref, na_ref, nm_ref, wg_ref,
                 wq_hbm, wk_hbm, wv_hbm, wo_hbm, w_in_hbm, w_out_hbm,
                 out_hbm, loss_ref, recv_hbm, ret_hbm,
                 wa_ref, wg3_ref, qkv_ref, ctx_ref, hbuf, obuf, aux_ref, lacc, lbuf, xs_ref,
                 w_in, w_out, mid_ref, lhs_ref, retb,
                 wa_sem, wf_sem, h_sem, o_sem, l_sem, r_sem, own_sem, own2_sem,
                 send_sem, recv_sem, send2_sem, recv2_sem, lsend_sem, lrecv_sem):
    me = lax.axis_index("ep")
    t = pl.program_id(0)
    seq, d = tok_ref.shape[1], tok_ref.shape[2]
    experts = wg_ref.shape[0]
    e_loc, _, ff = w_in.shape
    rows = e_loc * cap
    ks = peer_order(n)

    def wa_copy(i):
        return pltpu.make_async_copy((wq_hbm, wk_hbm, wv_hbm, wo_hbm)[i], wa_ref.at[i], wa_sem.at[i])

    def wf_copy(i):
        src, dst = ((w_in_hbm, w_in), (w_out_hbm, w_out))[i]
        return pltpu.make_async_copy(src, dst, wf_sem.at[i])

    def h_copy(i):
        return pltpu.make_async_copy(hbuf.at[lax.rem(i, 2)], out_hbm.at[i], h_sem.at[lax.rem(i, 2)])

    def h_back(i):
        return pltpu.make_async_copy(out_hbm.at[i], hbuf.at[lax.rem(i, 2)], h_sem.at[lax.rem(i, 2)])

    def o_copy(i):
        return pltpu.make_async_copy(obuf.at[lax.rem(i, 2)], out_hbm.at[i], o_sem.at[lax.rem(i, 2)])

    def lhs_copy(i):
        return pltpu.make_async_copy(recv_hbm.at[:, i], lhs_ref, l_sem)

    def ret_copy(i):
        return pltpu.make_async_copy(ret_hbm.at[i], retb.at[lax.rem(i, 2)], r_sem.at[lax.rem(i, 2)])

    def own_copy(i):
        return pltpu.make_async_copy(xs_ref.at[i, me], recv_hbm.at[me, i], own_sem.at[i])

    def own2_copy(i):
        return pltpu.make_async_copy(xs_ref.at[i, me], ret_hbm.at[i, me], own2_sem.at[i])

    def wait_peers(i, sem):
        block = xs_ref.at[i, pl.ds(0, n - 1)]
        pltpu.make_async_copy(block, block, sem.at[i]).wait()

    @pl.when(t == 0)
    def _():
        for i in range(4):
            wa_copy(i).start()
        barrier = pltpu.get_barrier_semaphore()
        for k in ks:
            pl.semaphore_signal(barrier, inc=1, device_id=(me ^ k,), device_id_type=MESH)
        lacc[...] = jnp.zeros_like(lacc)
        w = wg_ref[...]
        hi = w.astype(BF16)
        rest = w - hi.astype(F32)
        mid = rest.astype(BF16)
        wg3_ref[0:experts] = hi
        wg3_ref[experts:2 * experts] = mid
        wg3_ref[2 * experts:] = (rest - mid.astype(F32)).astype(BF16)

    @pl.when(t == 1)
    def _():
        pl.semaphore_wait(pltpu.get_barrier_semaphore(), n - 1)
        wf_copy(0).start()
        wf_copy(1).start()

    @pl.when((t > 0) & (t <= groups))
    def _():
        p = t - 1
        for k in ks:
            peer = me ^ k
            pltpu.make_async_remote_copy(
                src_ref=xs_ref.at[p, peer], dst_ref=recv_hbm.at[me, p],
                send_sem=send_sem.at[p], recv_sem=recv_sem.at[p],
                device_id=(peer,), device_id_type=MESH).start()
        own_copy(p).start()

    @pl.when(t == groups)
    def _():
        for k in ks:
            pltpu.make_async_remote_copy(
                src_ref=lacc, dst_ref=lbuf.at[me], send_sem=lsend_sem, recv_sem=lrecv_sem,
                device_id=(me ^ k,), device_id_type=MESH).start()
        lbuf[me] = lacc[...]
        h_copy(groups - 2).wait()
        h_copy(groups - 1).wait()
        wf_copy(0).wait()
        wf_copy(1).wait()

    @pl.when((t > groups) & (t <= 2 * groups))
    def _():
        p = t - groups - 1
        for k in ks:
            peer = me ^ k
            pltpu.make_async_remote_copy(
                src_ref=xs_ref.at[p, peer], dst_ref=ret_hbm.at[p, me],
                send_sem=send2_sem.at[p], recv_sem=recv2_sem.at[p],
                device_id=(peer,), device_id_type=MESH).start()
        own2_copy(p).start()

    @pl.when(t < groups)
    def _():
        g = t
        a = norm_rows(tok_ref[0].astype(F32), na_ref[...])
        for c in range(3):
            @pl.when(t == 0)
            def _():
                wa_copy(c).wait()
            qkv_ref[:, c * d:(c + 1) * d] = dot_nt(a, wa_ref[c]).astype(BF16)
        key_ok = mask_ref[pl.ds(g, 1), :] == 1
        low = lax.broadcasted_iota(jnp.int32, (seq, 128), 1) < 64
        factor = 0.125 * LOG2E

        def probs(q, k):
            s = jnp.where(key_ok, dot_nt(q, k), -1e30)
            e = jnp.exp2((s - jnp.max(s, axis=-1, keepdims=True)) * factor)
            return (e * (1.0 / jnp.sum(e, axis=-1, keepdims=True))).astype(BF16)

        def pair(i, carry):
            off = pl.multiple_of(i * 128, 128)
            q = qkv_ref[:, pl.ds(off, 128)]
            k = qkv_ref[:, pl.ds(pl.multiple_of(d + off, 128), 128)]
            v = qkv_ref[:, pl.ds(pl.multiple_of(2 * d + off, 128), 128)]
            zero = jnp.zeros_like(q)
            p0 = probs(jnp.where(low, q, zero), k)
            p1 = probs(jnp.where(low, zero, q), k)
            c = dot_nn(p0, jnp.where(low, v, zero))
            c += dot_nn(p1, jnp.where(low, zero, v))
            ctx_ref[:, pl.ds(off, 128)] = c.astype(BF16)
            return carry

        lax.fori_loop(0, heads // 2, pair, 0, unroll=2)

        @pl.when(t == 0)
        def _():
            wa_copy(3).wait()

        @pl.when(t >= 2)
        def _():
            h_copy(g - 2).wait()
        h = (tok_ref[0].astype(F32) + dot_nn(ctx_ref[...], wa_ref[3])).astype(BF16)
        hbuf[lax.rem(g, 2)] = h
        b = norm_rows(h.astype(F32), nm_ref[...])

        lg = dot_nt(wg3_ref[...], b)
        lg = lg[:experts] + (lg[experts:2 * experts] + lg[2 * experts:])
        ex = jnp.exp(lg - jnp.max(lg, axis=0, keepdims=True))
        p = ex / jnp.sum(ex, axis=0, keepdims=True)
        c1 = pick_ref[0, 0:1, :].astype(F32)
        c2 = pick_ref[0, 1:2, :].astype(F32)
        draw = draw_ref[pl.ds(g, 1), :]
        valid = jnp.where(key_ok, 1.0, 0.0)
        ids = lax.broadcasted_iota(jnp.int32, (experts, seq), 0).astype(F32)
        hot1 = jnp.where(ids == c1, 1.0, 0.0)
        hot2 = jnp.where(ids == c2, 1.0, 0.0)
        p1 = jnp.sum(hot1 * p, axis=0, keepdims=True)
        p2 = jnp.sum(hot2 * p, axis=0, keepdims=True)
        g1 = p1 / (p1 + p2)
        g2 = p2 / (p1 + p2)
        want2 = valid * jnp.where(draw < 2.0 * g2, 1.0, 0.0)
        take1 = hot1 * valid
        take2 = hot2 * want2
        upper = jnp.where(lax.broadcasted_iota(jnp.int32, (seq, seq), 0)
                          <= lax.broadcasted_iota(jnp.int32, (seq, seq), 1), 1.0, 0.0).astype(BF16)
        cum1 = dot_nn(take1.astype(BF16), upper)
        cum2 = dot_nn(take2.astype(BF16), upper)
        count1 = jnp.sum(take1, axis=1, keepdims=True)
        pos1 = jnp.sum((cum1 - 1.0) * take1, axis=0, keepdims=True)
        pos2 = jnp.sum((cum2 - 1.0 + jnp.minimum(count1, float(cap))) * take2, axis=0, keepdims=True)
        slot1 = jnp.where((valid > 0.5) & (pos1 < float(cap)), c1 * float(cap) + pos1, -1.0)
        slot2 = jnp.where((want2 > 0.5) & (pos2 < float(cap)), c2 * float(cap) + pos2, -1.0)
        half = experts * cap // 2
        for part in range(2):
            slots = lax.broadcasted_iota(jnp.int32, (half, seq), 0).astype(F32) + float(part * half)
            pick = jnp.where((slots == slot1) | (slots == slot2), 1.0, 0.0).astype(BF16)
            xs_ref[g, part * (n // 2):(part + 1) * (n // 2)] = dot_nn(pick, b).astype(BF16).reshape(n // 2, rows, d)
        density = jnp.sum(p * valid, axis=1, keepdims=True) * (1.0 / seq)
        lacc[...] += jnp.sum(count1 * (1.0 / seq) * density, axis=0, keepdims=True)
        aux_ref[g] = jnp.concatenate([slot1, slot2, g1, g2, g1, g1, g1, g1], axis=0)
        h_copy(g).start()

    @pl.when((t >= groups) & (t < 2 * groups))
    def _():
        r = t - groups
        wait_peers(r, recv_sem)
        own_copy(r).wait()
        lhs_copy(r).start()
        wait_peers(r, send_sem)
        lhs_copy(r).wait()
        for e in range(e_loc):
            lhs = lhs_ref[:, e * cap:(e + 1) * cap, :].reshape(n * cap, d)
            for c in range(2):
                cols = slice(c * (ff // 2), (c + 1) * (ff // 2))
                mid_ref[:, cols] = jnp.maximum(dot_nn(lhs, w_in[e, :, cols]), 0.0).astype(BF16)
            for c in range(2):
                cols = slice(c * (d // 2), (c + 1) * (d // 2))
                down = dot_nn(mid_ref[...], w_out[e, :, cols]).astype(BF16)
                xs_ref[r, :, e * cap:(e + 1) * cap, cols] = down.reshape(n, cap, d // 2)

    @pl.when((t >= 2 * groups) & (t < 3 * groups))
    def _():
        g = t - 2 * groups
        wait_peers(g, recv2_sem)
        own2_copy(g).wait()
        ret_copy(g).start()
        h_back(g).start()

    @pl.when(t > 2 * groups)
    def _():
        g = t - 2 * groups - 1
        slot1 = aux_ref[g, 0:1, :]
        slot2 = aux_ref[g, 1:2, :]
        g1 = aux_ref[g, 2:3, :]
        g2 = aux_ref[g, 3:4, :]
        ids = lax.broadcasted_iota(jnp.int32, (n * rows, seq), 0).astype(F32)
        comb = (jnp.where(ids == slot1, g1, 0.0) + jnp.where(ids == slot2, g2, 0.0)).astype(BF16)

        @pl.when(g >= 2)
        def _():
            o_copy(g - 2).wait()
        ret_copy(g).wait()
        h_back(g).wait()
        b = lax.rem(g, 2)
        moe = dot_tn(comb, retb[b].reshape(n * rows, d))
        obuf[b] = (hbuf[b].astype(F32) + moe).astype(BF16)
        o_copy(g).start()

    @pl.when(t == 3 * groups)
    def _():
        o_copy(groups - 2).wait()
        o_copy(groups - 1).wait()
        for i in range(groups):
            wait_peers(i, send2_sem)
        block = lbuf.at[pl.ds(0, n - 1)]
        pltpu.make_async_copy(block, block, lsend_sem).wait()
        pltpu.make_async_copy(block, block, lrecv_sem).wait()
        total = jnp.sum(lbuf[...], axis=0)
        loss_ref[...] = total[0:1, 0:1] * float(experts) / float(groups * n)


def solution(mesh):
    n = mesh.shape["ep"]

    def local_step(tokens, pad_mask, second_draw, choices, norm_attn, w_query, w_key, w_value, w_attn_out, norm_moe, w_gate, w_in, w_out):
        groups, seq, d = tokens.shape
        heads = w_query.shape[1]
        experts = w_gate.shape[1]
        e_loc, _, ff = w_in.shape
        cap = (2 * seq + experts - 1) // experts
        rows = e_loc * cap
        turned = [jnp.transpose(w, (1, 2, 0)).reshape(d, d) for w in (w_query, w_key, w_value)]
        wo = w_attn_out.reshape(d, d)
        last = groups - 1
        hbm = pl.BlockSpec(memory_space=pl.ANY)

        def whole(shape):
            return pl.BlockSpec(shape, lambda t: (0,) * len(shape), pipeline_mode=pl.Buffered(1))

        dma = pltpu.SemaphoreType.DMA
        out, loss, _, _ = pl.pallas_call(
            functools.partial(layer_kernel, n, heads, cap, groups),
            grid=(3 * groups + 1,),
            out_shape=(jax.ShapeDtypeStruct((groups, seq, d), BF16),
                       jax.ShapeDtypeStruct((1, 1), F32),
                       jax.ShapeDtypeStruct((n, groups, rows, d), BF16),
                       jax.ShapeDtypeStruct((groups, n, rows, d), BF16)),
            in_specs=[whole((groups, seq)), whole((groups, seq)),
                      pl.BlockSpec((1, 2, seq), lambda t: (jnp.minimum(t, last), 0, 0)),
                      pl.BlockSpec((1, seq, d), lambda t: (jnp.minimum(t, last), 0, 0)),
                      whole((1, d)), whole((1, d)), whole((experts, d))] + [hbm] * 6,
            out_specs=(hbm, pl.BlockSpec((1, 1), lambda t: (0, 0)), hbm, hbm),
            scratch_shapes=[pltpu.VMEM((4, d, d), BF16), pltpu.VMEM((3 * experts, d), BF16),
                            pltpu.VMEM((seq, 3 * d), BF16), pltpu.VMEM((seq, d), BF16),
                            pltpu.VMEM((2, seq, d), BF16), pltpu.VMEM((2, seq, d), BF16),
                            pltpu.VMEM((groups, 8, seq), F32), pltpu.VMEM((8, 128), F32),
                            pltpu.VMEM((n, 8, 128), F32), pltpu.VMEM((groups, n, rows, d), BF16),
                            pltpu.VMEM((e_loc, d, ff), BF16), pltpu.VMEM((e_loc, ff, d), BF16),
                            pltpu.VMEM((n * cap, ff), BF16), pltpu.VMEM((n, rows, d), BF16),
                            pltpu.VMEM((2, n, rows, d), BF16),
                            dma((4,)), dma((2,)), dma((2,)), dma((2,)), dma, dma((2,)),
                            dma((groups,)), dma((groups,)), dma((groups,)), dma((groups,)),
                            dma((groups,)), dma((groups,)), dma, dma],
            compiler_params=pltpu.CompilerParams(collective_id=0, has_side_effects=True,
                                                 vmem_limit_bytes=67043328),
        )(pad_mask, second_draw, jnp.transpose(choices, (0, 2, 1)), tokens,
          norm_attn.reshape(1, d), norm_moe.reshape(1, d), w_gate.T, *turned, wo, w_in, w_out)
        return out, loss[0, 0]

    by_group = P("ep")
    replicated = P()
    in_specs = (by_group, by_group, by_group, by_group, replicated, replicated, replicated, replicated, replicated, replicated, replicated, by_group, by_group)
    return jax.shard_map(local_step, mesh=mesh, in_specs=in_specs, out_specs=(by_group, replicated), check_vma=False)
```

time: 918 us -> 400 us (0.44)
  blocking collectives: 425 us -> 0 us
  Pallas kernels: 0 us -> 384 us
  matrix products: 268 us -> 0 us
  other arithmetic: 96.8 us -> 0 us
  local copies, waits for them, and re-layouts: 102 us -> 8.12 us
  starting transfers between devices: 13.6 us -> 0 us
    pallas_call x0 -> x1, Pallas kernels: none -> 384 us  [local_step(): pl.pallas_call(functools.partial(layer_kernel, n, heads, cap, groups), gr...]
    dot_general x10 -> x0, matrix products: 268 us -> none  [the longest x1 72.1 us: local_step(): jnp.einsum('egcd,edf->egcf', received, w_in, preferred_element_type=jnp.f...]
    psum x1 -> x0, blocking collectives: 231 us -> none  [local_step(): aux_loss = lax.psum(aux_sum, 'ep') * experts / (groups_local * n_dev)]
    all_to_all x1 -> x0, blocking collectives: 194 us -> none  [local_step(): received = lax.all_to_all(send_buf, 'ep', 0, 1, tiled=True)]
    sub x1 -> x0, other arithmetic: 68.7 us -> none  [attention_block(): attn_probs = jax.nn.softmax(scores, axis=-1).astype(jnp.bfloat16)]
    all_to_all x3 -> x0, local copies, waits for them, and re-layouts: 62.7 us -> none  [the longest x2 56.1 us: local_step(): returned = lax.all_to_all(expert_out, 'ep', 1, 0, tiled=True)]
    convert_element_type x2 -> x0, local copies, waits for them, and re-layouts: 34.1 us -> none  [the longest x1 18.7 us: local_step(): jnp.einsum('egcf,efd->egcd', inner_act, w_out, preferred_element_type=jnp...]
    another operation x4 -> x0, other arithmetic: 18.6 us -> none
  transfers between devices with their start and end apart: 1 -> 0, of which waited for: 0 -> 0; matrix products, arithmetic and copies ran while one was open for 0% -> 0% of each run, Pallas kernels for 0% -> 0%
where the time goes in v2:
time: 400 us; the launch traced here: 395 us
  Pallas kernels  384 us (96%)
  local copies, waits for them, and re-layouts  8.12 us (2%)
    pallas_call x1, Pallas kernels, local_step(): pl.pallas_call(functools.partial(layer_kernel, n, heads, cap, groups), gr...  384 us
    unnamed x1, local copies, waits for them, and re-layouts  8.12 us

profile of v2, /device:TPU:0, one launch (start us, length us, event | category | flops | bytes accessed | tf_op | source)
XLA Modules:
  0.0 394.9 jit_solution(14915602057051318494)
XLA Ops:
  0.6 384.3 %shard_map.140 = (bf16[16,256,1024]{2,1,0:T(8,128)(2,1)}, f32[1,1]{1,0:T(1,128)}, bf16[16,16,32,1024]{3,2,1,0:T(8,128)(2,1)}, bf16[16,16,32,1024]{3,2,1,0:T(8,128)(2,1)}) custom-call(s32[16,256]{1,0:T(8,128)} %mask_ref.1, f32[16,256]{1,0:T(8,128)} %draw_ref.1, s32[16,2,256]{2,1,0:T(2,128)} %bitcast.20, bf16[16,256,1024]{2,1,0:T(8,128)(2,1)} %tok_ref.1, ...), custom_call_target="tpu_custom_call" | custom-call | tf_op jit(solution)/shard_map/pallas_call | solution.py:300
  385.0 8.1 %copy.17 = bf16[16,256,1024]{2,1,0:T(8,128)(2,1)} copy(bf16[16,256,1024]{2,1,0:T(8,128)(2,1)} %get-tuple-element.8) | data formatting | bytes 16777216

commit v3 on v2

--- a/solution.py
+++ b/solution.py
@@ -11,6 +11,8 @@
 F32 = jnp.float32
 BF16 = jnp.bfloat16
 LOG2E = 1.4426950408889634
+O_ROUNDS = 5
+INNER = 3
 
 
 def norm_rows(x, scale):
@@ -33,6 +35,61 @@
 def peer_order(n):
     full = [2, 4, 8, 3, 5, 9, 6, 12, 10, 7, 13, 11, 14, 15, 1]
     return full if n == 16 else list(range(1, n))
+
+
+def attend_heads(qkv_ref, ctx_ref, key_ok, heads):
+    seq, d = ctx_ref.shape
+    low = lax.broadcasted_iota(jnp.int32, (seq, 128), 1) < 64
+    factor = 0.125 * LOG2E
+
+    def probs(q, k):
+        s = jnp.where(key_ok, dot_nt(q, k), -1e30)
+        e = jnp.exp2((s - jnp.max(s, axis=-1, keepdims=True)) * factor)
+        return (e * (1.0 / jnp.sum(e, axis=-1, keepdims=True))).astype(BF16)
+
+    def pair(i, carry):
+        off = pl.multiple_of(i * 128, 128)
+        q = qkv_ref[:, pl.ds(off, 128)]
+        k = qkv_ref[:, pl.ds(pl.multiple_of(d + off, 128), 128)]
+        v = qkv_ref[:, pl.ds(pl.multiple_of(2 * d + off, 128), 128)]
+        zero = jnp.zeros_like(q)
+        p0 = probs(jnp.where(low, q, zero), k)
+        p1 = probs(jnp.where(low, zero, q), k)
+        c = dot_nn(p0, jnp.where(low, v, zero))
+        c += dot_nn(p1, jnp.where(low, zero, v))
+        ctx_ref[:, pl.ds(off, 128)] = c.astype(BF16)
+        return carry
+
+    lax.fori_loop(0, heads // 2, pair, 0, unroll=4)
+
+
+def gate(wg3_ref, b, pick_ref, draw, key_ok, cap):
+    experts, seq = wg3_ref.shape[0] // 3, b.shape[0]
+    lg = dot_nt(wg3_ref[...], b)
+    lg = lg[:experts] + (lg[experts:2 * experts] + lg[2 * experts:])
+    ex = jnp.exp(lg - jnp.max(lg, axis=0, keepdims=True))
+    p = ex / jnp.sum(ex, axis=0, keepdims=True)
+    c1 = pick_ref[0, 0:1, :].astype(F32)
+    c2 = pick_ref[0, 1:2, :].astype(F32)
+    valid = jnp.where(key_ok, 1.0, 0.0)
+    ids = lax.broadcasted_iota(jnp.int32, (experts, seq), 0).astype(F32)
+    hot1 = jnp.where(ids == c1, 1.0, 0.0)
+    hot2 = jnp.where(ids == c2, 1.0, 0.0)
+    p1 = jnp.sum(hot1 * p, axis=0, keepdims=True)
+    p2 = jnp.sum(hot2 * p, axis=0, keepdims=True)
+    g1 = p1 / (p1 + p2)
+    g2 = p2 / (p1 + p2)
+    want2 = valid * jnp.where(draw < 2.0 * g2, 1.0, 0.0)
+    take1 = hot1 * valid
+    take2 = hot2 * want2
+    upper = jnp.where(lax.broadcasted_iota(jnp.int32, (seq, seq), 0)
+                      <= lax.broadcasted_iota(jnp.int32, (seq, seq), 1), 1.0, 0.0).astype(BF16)
+    cum1 = dot_nn(take1.astype(BF16), upper)
+    cum2 = dot_nn(take2.astype(BF16), upper)
+    count1 = jnp.sum(take1, axis=1, keepdims=True)
+    pos1 = jnp.sum((cum1 - 1.0) * take1, axis=0, keepdims=True)
+    pos2 = jnp.sum((cum2 - 1.0 + jnp.minimum(count1, float(cap))) * take2, axis=0, keepdims=True)
+    return p, c1, c2, valid, hot1, hot2, g1, g2, want2, take2, count1, pos1, pos2
 
 
 def layer_kernel(n, heads, cap, groups, mask_ref, draw_ref, pick_ref, tok_ref, na_ref, nm_ref, wg_ref,
@@ -148,28 +205,7 @@
                 wa_copy(c).wait()
             qkv_ref[:, c * d:(c + 1) * d] = dot_nt(a, wa_ref[c]).astype(BF16)
         key_ok = mask_ref[pl.ds(g, 1), :] == 1
-        low = lax.broadcasted_iota(jnp.int32, (seq, 128), 1) < 64
-        factor = 0.125 * LOG2E
-
-        def probs(q, k):
-            s = jnp.where(key_ok, dot_nt(q, k), -1e30)
-            e = jnp.exp2((s - jnp.max(s, axis=-1, keepdims=True)) * factor)
-            return (e * (1.0 / jnp.sum(e, axis=-1, keepdims=True))).astype(BF16)
-
-        def pair(i, carry):
-            off = pl.multiple_of(i * 128, 128)
-            q = qkv_ref[:, pl.ds(off, 128)]
-            k = qkv_ref[:, pl.ds(pl.multiple_of(d + off, 128), 128)]
-            v = qkv_ref[:, pl.ds(pl.multiple_of(2 * d + off, 128), 128)]
-            zero = jnp.zeros_like(q)
-            p0 = probs(jnp.where(low, q, zero), k)
-            p1 = probs(jnp.where(low, zero, q), k)
-            c = dot_nn(p0, jnp.where(low, v, zero))
-            c += dot_nn(p1, jnp.where(low, zero, v))
-            ctx_ref[:, pl.ds(off, 128)] = c.astype(BF16)
-            return carry
-
-        lax.fori_loop(0, heads // 2, pair, 0, unroll=2)
+        attend_heads(qkv_ref, ctx_ref, key_ok, heads)
 
         @pl.when(t == 0)
         def _():
@@ -182,31 +218,8 @@
         hbuf[lax.rem(g, 2)] = h
         b = norm_rows(h.astype(F32), nm_ref[...])
 
-        lg = dot_nt(wg3_ref[...], b)
-        lg = lg[:experts] + (lg[experts:2 * experts] + lg[2 * experts:])
-        ex = jnp.exp(lg - jnp.max(lg, axis=0, keepdims=True))
-        p = ex / jnp.sum(ex, axis=0, keepdims=True)
-        c1 = pick_ref[0, 0:1, :].astype(F32)
-        c2 = pick_ref[0, 1:2, :].astype(F32)
-        draw = draw_ref[pl.ds(g, 1), :]
-        valid = jnp.where(key_ok, 1.0, 0.0)
-        ids = lax.broadcasted_iota(jnp.int32, (experts, seq), 0).astype(F32)
-        hot1 = jnp.where(ids == c1, 1.0, 0.0)
-        hot2 = jnp.where(ids == c2, 1.0, 0.0)
-        p1 = jnp.sum(hot1 * p, axis=0, keepdims=True)
-        p2 = jnp.sum(hot2 * p, axis=0, keepdims=True)
-        g1 = p1 / (p1 + p2)
-        g2 = p2 / (p1 + p2)
-        want2 = valid * jnp.where(draw < 2.0 * g2, 1.0, 0.0)
-        take1 = hot1 * valid
-        take2 = hot2 * want2
-        upper = jnp.where(lax.broadcasted_iota(jnp.int32, (seq, seq), 0)
-                          <= lax.broadcasted_iota(jnp.int32, (seq, seq), 1), 1.0, 0.0).astype(BF16)
-        cum1 = dot_nn(take1.astype(BF16), upper)
-        cum2 = dot_nn(take2.astype(BF16), upper)
-        count1 = jnp.sum(take1, axis=1, keepdims=True)
-        pos1 = jnp.sum((cum1 - 1.0) * take1, axis=0, keepdims=True)
-        pos2 = jnp.sum((cum2 - 1.0 + jnp.minimum(count1, float(cap))) * take2, axis=0, keepdims=True)
+        p, c1, c2, valid, hot1, hot2, g1, g2, want2, take2, count1, pos1, pos2 = gate(
+            wg3_ref, b, pick_ref, draw_ref[pl.ds(g, 1), :], key_ok, cap)
         slot1 = jnp.where((valid > 0.5) & (pos1 < float(cap)), c1 * float(cap) + pos1, -1.0)
         slot2 = jnp.where((want2 > 0.5) & (pos2 < float(cap)), c2 * float(cap) + pos2, -1.0)
         half = experts * cap // 2
@@ -278,6 +291,304 @@
         loss_ref[...] = total[0:1, 0:1] * float(experts) / float(groups * n)
 
 
+def packed_kernel(n, heads, cap, groups, s_rounds, o_rounds, inner, mask_ref, draw_ref, pick_ref, tok_ref, na_ref, nm_ref, wg_ref,
+                  wq_hbm, wk_hbm, wv_hbm, wo_hbm, w_in_hbm, w_out_hbm,
+                  out_hbm, loss_ref, flag_ref, recv_hbm, ret_hbm,
+                  wa_ref, wg3_ref, qkv_ref, ctx_ref, hbuf, acc_ref, aux_ref, base_ref, lacc, lbuf, xs_ref, ball_ref,
+                  w_in, w_out,
+                  wa_sem, wf_sem, h_sem, o_sem, l_sem, r_sem, own_sem, own2_sem,
+                  send_sem, recv_sem, send2_sem, recv2_sem, lsend_sem, lrecv_sem):
+    me = lax.axis_index("ep")
+    t = pl.program_id(0)
+    seq, d = tok_ref.shape[1], tok_ref.shape[2]
+    experts = wg_ref.shape[0]
+    e_loc, _, ff = w_in.shape
+    rows = e_loc * cap
+    full = n * rows
+    low_cap = cap // 2
+    rounds = s_rounds + o_rounds
+    t_over = 3 * s_rounds
+    t_ffn = t_over + o_rounds
+    t_comb = t_ffn + rounds - inner
+    couple, part_of = t // 3, lax.rem(t, 3)
+    in_front = t < t_over
+    over_max = float(o_rounds * cap)
+    ks = peer_order(n)
+
+    def my_rows(i):
+        return pl.ds(pl.multiple_of(i * rows, rows), rows)
+
+    def wa_copy(i):
+        return pltpu.make_async_copy((wq_hbm, wk_hbm, wv_hbm, wo_hbm)[i], wa_ref.at[i], wa_sem.at[i])
+
+    def wf_copy(i):
+        src, dst = ((w_in_hbm, w_in), (w_out_hbm, w_out))[i]
+        return pltpu.make_async_copy(src, dst, wf_sem.at[i])
+
+    def h_copy(i):
+        b = lax.rem(i, 2)
+        return pltpu.make_async_copy(hbuf.at[b, 0], out_hbm.at[i], h_sem.at[b])
+
+    def h_back(i):
+        b = lax.rem(i, 2)
+        return pltpu.make_async_copy(out_hbm.at[pl.ds(2 * i, 2)], hbuf.at[b], h_sem.at[b])
+
+    def o_copy(i):
+        b = lax.rem(i, 2)
+        return pltpu.make_async_copy(hbuf.at[b], out_hbm.at[pl.ds(2 * i, 2)], o_sem.at[b])
+
+    def lhs_copy(i):
+        return [pltpu.make_async_copy(recv_hbm.at[i, pl.ds(b * seq, seq)], hbuf.at[b, 1], l_sem.at[b]) for b in range(2)]
+
+    def ret_copy(i):
+        return pltpu.make_async_copy(ret_hbm.at[i], wa_ref.at[1, pl.ds(0, full)], r_sem)
+
+    def over_copy(i):
+        return pltpu.make_async_copy(ret_hbm.at[s_rounds + i], ball_ref.at[pl.ds(i * full, full)], wa_sem.at[0])
+
+    def own_copy(i):
+        return pltpu.make_async_copy(xs_ref.at[i, me], recv_hbm.at[i, my_rows(me)], own_sem.at[i])
+
+    def own2_copy(i):
+        return pltpu.make_async_copy(xs_ref.at[i, me], ret_hbm.at[i, my_rows(me)], own2_sem.at[i])
+
+    def wait_peers(i, sem):
+        block = xs_ref.at[i, pl.ds(0, n - 1)]
+        pltpu.make_async_copy(block, block, sem.at[i]).wait()
+
+    def round_of(i):
+        return jnp.where(i < 1, inner, jnp.where(i <= o_rounds, i - 1 + s_rounds, i - o_rounds + inner))
+
+    def inner_of(c):
+        return (c >= 2) & (c < 2 + inner)
+
+    def row_ids(count, start):
+        return (lax.broadcasted_iota(jnp.int32, (count, seq), 0) + start).astype(F32)
+
+    def pick_rows(ids, g, first):
+        one = aux_ref[g, first:first + 1, :]
+        two = aux_ref[g, first + 1:first + 2, :]
+        return jnp.where((ids == one) | (ids == two), 1.0, 0.0).astype(BF16)
+
+    def gate_rows(ids, g, first):
+        one = aux_ref[g, first:first + 1, :]
+        two = aux_ref[g, first + 1:first + 2, :]
+        return (jnp.where(ids == one, aux_ref[g, 4:5, :], 0.0)
+                + jnp.where(ids == two, aux_ref[g, 5:6, :], 0.0)).astype(BF16)
+
+    @pl.when(t == 0)
+    def _():
+        for i in range(4):
+            wa_copy(i).start()
+        barrier = pltpu.get_barrier_semaphore()
+        for k in ks:
+            pl.semaphore_signal(barrier, inc=1, device_id=(me ^ k,), device_id_type=MESH)
+        lacc[...] = jnp.zeros_like(lacc)
+        base_ref[...] = jnp.zeros_like(base_ref)
+        w = wg_ref[...]
+        hi = w.astype(BF16)
+        rest = w - hi.astype(F32)
+        mid = rest.astype(BF16)
+        wg3_ref[0:experts] = hi
+        wg3_ref[experts:2 * experts] = mid
+        wg3_ref[2 * experts:] = (rest - mid.astype(F32)).astype(BF16)
+
+    @pl.when(t == 1)
+    def _():
+        pl.semaphore_wait(pltpu.get_barrier_semaphore(), n - 1)
+        wf_copy(0).start()
+        wf_copy(1).start()
+
+    @pl.when((in_front & (part_of == 2)) | ((t > t_over) & (t <= t_ffn)))
+    def _():
+        p = jnp.where(in_front, couple, t - t_over - 1 + s_rounds)
+        for k in ks:
+            peer = me ^ k
+            pltpu.make_async_remote_copy(
+                src_ref=xs_ref.at[p, peer], dst_ref=recv_hbm.at[p, my_rows(me)],
+                send_sem=send_sem.at[p], recv_sem=recv_sem.at[p],
+                device_id=(peer,), device_id_type=MESH).start()
+        own_copy(p).start()
+
+    @pl.when(t == t_over)
+    def _():
+        over = jnp.sum(jnp.where(base_ref[:, 0:1] > over_max, 1.0, 0.0), axis=0, keepdims=True)
+        top = lax.broadcasted_iota(jnp.int32, lacc.shape, 0) < 4
+        lacc[...] = jnp.where(top, lacc[...], over)
+        h_copy(groups - 2).wait()
+        h_copy(groups - 1).wait()
+
+    @pl.when(t == 8)
+    def _():
+        wf_copy(0).wait()
+        wf_copy(1).wait()
+
+    @pl.when(t == t_over + 1)
+    def _():
+        for k in ks:
+            pltpu.make_async_remote_copy(
+                src_ref=lacc, dst_ref=lbuf.at[me], send_sem=lsend_sem, recv_sem=lrecv_sem,
+                device_id=(me ^ k,), device_id_type=MESH).start()
+        lbuf[me] = lacc[...]
+
+    @pl.when((in_front & (part_of == 0) & inner_of(couple - 1)) | ((t > t_ffn) & (t <= t_comb)))
+    def _():
+        p = jnp.where(in_front, couple - 3, round_of(t - t_ffn - 1))
+        for k in ks:
+            peer = me ^ k
+            pltpu.make_async_remote_copy(
+                src_ref=xs_ref.at[p, peer], dst_ref=ret_hbm.at[p, my_rows(me)],
+                send_sem=send2_sem.at[p], recv_sem=recv2_sem.at[p],
+                device_id=(peer,), device_id_type=MESH).start()
+        own2_copy(p).start()
+
+    @pl.when(in_front & (part_of < 2))
+    def _():
+        g = 2 * couple + part_of
+        a = norm_rows(tok_ref[0].astype(F32), na_ref[...])
+        for c in range(3):
+            @pl.when(t == 0)
+            def _():
+                wa_copy(c).wait()
+            qkv_ref[:, c * d:(c + 1) * d] = dot_nt(a, wa_ref[c]).astype(BF16)
+        key_ok = mask_ref[pl.ds(g, 1), :] == 1
+        attend_heads(qkv_ref, ctx_ref, key_ok, heads)
+
+        @pl.when(t == 0)
+        def _():
+            wa_copy(3).wait()
+
+        @pl.when(g >= 2)
+        def _():
+            h_copy(g - 2).wait()
+        h = (tok_ref[0].astype(F32) + dot_nn(ctx_ref[...], wa_ref[3])).astype(BF16)
+        hbuf[lax.rem(g, 2), 0] = h
+        b = norm_rows(h.astype(F32), nm_ref[...])
+        ball_ref[pl.ds(pl.multiple_of(g * seq, seq), seq), :] = b
+
+        p, c1, c2, valid, hot1, hot2, g1, g2, want2, take2, count1, pos1, pos2 = gate(
+            wg3_ref, b, pick_ref, draw_ref[pl.ds(g, 1), :], key_ok, cap)
+        keep1 = (valid > 0.5) & (pos1 < float(cap))
+        keep2 = (want2 > 0.5) & (pos2 < float(cap))
+        low = float(low_cap)
+        base = base_ref[:, 0:1]
+        parity = (lax.rem(g, 2) * low_cap).astype(F32)
+
+        def place(keep, hot, chosen, pos):
+            fixed = jnp.where(keep & (pos < low), chosen * float(cap) + parity + pos, -1.0)
+            q = jnp.sum(hot * base, axis=0, keepdims=True) + pos - low
+            block = jnp.floor(q * (1.0 / cap))
+            packed = block * float(full) + chosen * float(cap) + (q - block * float(cap))
+            return fixed, jnp.where(keep & (pos >= low) & (q < over_max), packed, -1.0)
+
+        s1, o1 = place(keep1, hot1, c1, pos1)
+        s2, o2 = place(keep2, hot2, c2, pos2)
+        kept = jnp.minimum(count1 + jnp.sum(take2, axis=1, keepdims=True), float(cap))
+        base_ref[...] += jnp.maximum(kept - low, 0.0)
+        aux_ref[g] = jnp.concatenate([s1, s2, o1, o2, g1, g2, g1, g1], axis=0)
+        density = jnp.sum(p * valid, axis=1, keepdims=True) * (1.0 / seq)
+        lacc[...] += jnp.sum(count1 * (1.0 / seq) * density, axis=0, keepdims=True)
+        h_copy(g).start()
+
+        @pl.when(part_of == 1)
+        def _():
+            both = ball_ref[pl.ds(pl.multiple_of((g - 1) * seq, seq), 2 * seq), :]
+            for part in range(2):
+                ids = row_ids(full // 2, part * (full // 2))
+                pick = jnp.concatenate([pick_rows(ids, g - 1, 0), pick_rows(ids, g, 0)], axis=1)
+                xs_ref[g // 2, part * (n // 2):(part + 1) * (n // 2)] = dot_nn(pick, both).astype(BF16).reshape(n // 2, rows, d)
+
+    @pl.when((t >= t_over) & (t < t_ffn))
+    def _():
+        j = t - t_over
+        quad = 4
+        for part in range(2):
+            ids = row_ids(full // 2, j * full + part * (full // 2))
+            acc_ref[...] = jnp.zeros_like(acc_ref)
+
+            def chunk(c, carry):
+                picks = [pick_rows(ids, c * quad + u, 2) for u in range(quad)]
+                span = ball_ref[pl.ds(pl.multiple_of(c * quad * seq, quad * seq), quad * seq), :]
+                acc_ref[0] += dot_nn(jnp.concatenate(picks, axis=1), span)
+                return carry
+
+            lax.fori_loop(0, groups // quad, chunk, 0)
+            xs_ref[s_rounds + j, part * (n // 2):(part + 1) * (n // 2)] = acc_ref[0].astype(BF16).reshape(n // 2, rows, d)
+
+    @pl.when((in_front & (part_of == 2) & inner_of(couple)) | ((t >= t_ffn) & (t < t_comb)))
+    def _():
+        r = jnp.where(in_front, couple - 2, round_of(t - t_ffn))
+        wait_peers(r, recv_sem)
+        own_copy(r).wait()
+        for copy in lhs_copy(r):
+            copy.start()
+        wait_peers(r, send_sem)
+        for copy in lhs_copy(r):
+            copy.wait()
+        for e in range(e_loc):
+            lhs = jnp.concatenate([hbuf[b, 1].reshape(n // 2, rows, d)[:, e * cap:(e + 1) * cap, :].reshape(seq // 2, d)
+                                   for b in range(2)], axis=0)
+            for c in range(2):
+                cols = slice(c * (ff // 2), (c + 1) * (ff // 2))
+                qkv_ref[:, cols] = jnp.maximum(dot_nn(lhs, w_in[e, :, cols]), 0.0).astype(BF16)
+            for c in range(2):
+                cols = slice(c * (d // 2), (c + 1) * (d // 2))
+                down = dot_nn(qkv_ref[:, 0:ff], w_out[e, :, cols]).astype(BF16)
+                xs_ref[r, :, e * cap:(e + 1) * cap, cols] = down.reshape(n, cap, d // 2)
+
+    @pl.when(t == t_comb)
+    def _():
+        for i in range(o_rounds):
+            wait_peers(s_rounds + i, recv2_sem)
+            own2_copy(s_rounds + i).wait()
+            over_copy(i).start()
+            over_copy(i).wait()
+
+    @pl.when(t >= t_comb)
+    def _():
+        i = t - t_comb
+
+        @pl.when(i >= 2)
+        def _():
+            o_copy(i - 2).wait()
+        h_back(i).start()
+        acc_ref[...] = jnp.zeros_like(acc_ref)
+
+        def both(start, first):
+            ids = row_ids(full, start)
+            return jnp.concatenate([gate_rows(ids, 2 * i + u, first) for u in range(2)], axis=1)
+
+        def chunk(c, carry):
+            moe = dot_tn(both(c * full, 2), ball_ref[pl.ds(pl.multiple_of(c * full, full), full), :])
+            acc_ref[...] += moe.reshape(2, seq, d)
+            return carry
+
+        lax.fori_loop(0, o_rounds, chunk, 0)
+        comb = both(0, 0)
+        wait_peers(i, recv2_sem)
+        own2_copy(i).wait()
+        ret_copy(i).start()
+        h_back(i).wait()
+        ret_copy(i).wait()
+        b = lax.rem(i, 2)
+        moe = acc_ref[...] + dot_tn(comb, wa_ref[1, 0:full]).reshape(2, seq, d)
+        hbuf[b] = (hbuf[b].astype(F32) + moe).astype(BF16)
+        o_copy(i).start()
+
+    @pl.when(t == t_comb + s_rounds - 1)
+    def _():
+        o_copy(s_rounds - 2).wait()
+        o_copy(s_rounds - 1).wait()
+        for i in range(rounds):
+            wait_peers(i, send2_sem)
+        block = lbuf.at[pl.ds(0, n - 1)]
+        pltpu.make_async_copy(block, block, lsend_sem).wait()
+        pltpu.make_async_copy(block, block, lrecv_sem).wait()
+        total = jnp.sum(lbuf[...], axis=0)
+        loss_ref[...] = total[0:1, 0:1] * float(experts) / float(groups * n)
+        flag_ref[...] = total[4:5, 0:1]
+
+
 def solution(mesh):
     n = mesh.shape["ep"]
 
@@ -297,36 +608,69 @@
             return pl.BlockSpec(shape, lambda t: (0,) * len(shape), pipeline_mode=pl.Buffered(1))
 
         dma = pltpu.SemaphoreType.DMA
-        out, loss, _, _ = pl.pallas_call(
-            functools.partial(layer_kernel, n, heads, cap, groups),
-            grid=(3 * groups + 1,),
+        operands = (pad_mask, second_draw, jnp.transpose(choices, (0, 2, 1)), tokens,
+                    norm_attn.reshape(1, d), norm_moe.reshape(1, d), w_gate.T, *turned, wo, w_in, w_out)
+
+        def group_blocks(group_of):
+            return [whole((groups, seq)), whole((groups, seq)),
+                    pl.BlockSpec((1, 2, seq), lambda t: (group_of(t), 0, 0)),
+                    pl.BlockSpec((1, seq, d), lambda t: (group_of(t), 0, 0)),
+                    whole((1, d)), whole((1, d)), whole((experts, d))] + [hbm] * 6
+
+        def full_layer():
+            return pl.pallas_call(
+                functools.partial(layer_kernel, n, heads, cap, groups),
+                grid=(3 * groups + 1,),
+                out_shape=(jax.ShapeDtypeStruct((groups, seq, d), BF16),
+                           jax.ShapeDtypeStruct((1, 1), F32),
+                           jax.ShapeDtypeStruct((n, groups, rows, d), BF16),
+                           jax.ShapeDtypeStruct((groups, n, rows, d), BF16)),
+                in_specs=group_blocks(lambda t: jnp.minimum(t, last)),
+                out_specs=(hbm, pl.BlockSpec((1, 1), lambda t: (0, 0)), hbm, hbm),
+                scratch_shapes=[pltpu.VMEM((4, d, d), BF16), pltpu.VMEM((3 * experts, d), BF16),
+                                pltpu.VMEM((seq, 3 * d), BF16), pltpu.VMEM((seq, d), BF16),
+                                pltpu.VMEM((2, seq, d), BF16), pltpu.VMEM((2, seq, d), BF16),
+                                pltpu.VMEM((groups, 8, seq), F32), pltpu.VMEM((8, 128), F32),
+                                pltpu.VMEM((n, 8, 128), F32), pltpu.VMEM((groups, n, rows, d), BF16),
+                                pltpu.VMEM((e_loc, d, ff), BF16), pltpu.VMEM((e_loc, ff, d), BF16),
+                                pltpu.VMEM((n * cap, ff), BF16), pltpu.VMEM((n, rows, d), BF16),
+                                pltpu.VMEM((2, n, rows, d), BF16),
+                                dma((4,)), dma((2,)), dma((2,)), dma((2,)), dma, dma((2,)),
+                                dma((groups,)), dma((groups,)), dma((groups,)), dma((groups,)),
+                                dma((groups,)), dma((groups,)), dma, dma],
+                compiler_params=pltpu.CompilerParams(collective_id=1, has_side_effects=True,
+                                                     vmem_limit_bytes=67043328),
+            )(*operands)[0]
+
+        s_rounds, o_rounds, inner = groups // 2, O_ROUNDS, INNER
+        rounds = s_rounds + o_rounds
+        scalar = pl.BlockSpec((1, 1), lambda t: (0, 0))
+        out, loss, flag, _, _ = pl.pallas_call(
+            functools.partial(packed_kernel, n, heads, cap, groups, s_rounds, o_rounds, inner),
+            grid=(3 * s_rounds + o_rounds + rounds - inner + s_rounds,),
             out_shape=(jax.ShapeDtypeStruct((groups, seq, d), BF16),
-                       jax.ShapeDtypeStruct((1, 1), F32),
-                       jax.ShapeDtypeStruct((n, groups, rows, d), BF16),
-                       jax.ShapeDtypeStruct((groups, n, rows, d), BF16)),
-            in_specs=[whole((groups, seq)), whole((groups, seq)),
-                      pl.BlockSpec((1, 2, seq), lambda t: (jnp.minimum(t, last), 0, 0)),
-                      pl.BlockSpec((1, seq, d), lambda t: (jnp.minimum(t, last), 0, 0)),
-                      whole((1, d)), whole((1, d)), whole((experts, d))] + [hbm] * 6,
-            out_specs=(hbm, pl.BlockSpec((1, 1), lambda t: (0, 0)), hbm, hbm),
+                       jax.ShapeDtypeStruct((1, 1), F32), jax.ShapeDtypeStruct((1, 1), F32),
+                       jax.ShapeDtypeStruct((rounds, n * rows, d), BF16),
+                       jax.ShapeDtypeStruct((rounds, n * rows, d), BF16)),
+            in_specs=group_blocks(lambda t: jnp.minimum(2 * (t // 3) + jnp.minimum(lax.rem(t, 3), 1), last)),
+            out_specs=(hbm, scalar, scalar, hbm, hbm),
             scratch_shapes=[pltpu.VMEM((4, d, d), BF16), pltpu.VMEM((3 * experts, d), BF16),
                             pltpu.VMEM((seq, 3 * d), BF16), pltpu.VMEM((seq, d), BF16),
-                            pltpu.VMEM((2, seq, d), BF16), pltpu.VMEM((2, seq, d), BF16),
-                            pltpu.VMEM((groups, 8, seq), F32), pltpu.VMEM((8, 128), F32),
-                            pltpu.VMEM((n, 8, 128), F32), pltpu.VMEM((groups, n, rows, d), BF16),
+                            pltpu.VMEM((2, 2, seq, d), BF16), pltpu.VMEM((2, seq, d), F32),
+                            pltpu.VMEM((groups, 8, seq), F32), pltpu.VMEM((experts, 128), F32),
+                            pltpu.VMEM((8, 128), F32), pltpu.VMEM((n, 8, 128), F32),
+                            pltpu.VMEM((rounds, n, rows, d), BF16), pltpu.VMEM((groups * seq, d), BF16),
                             pltpu.VMEM((e_loc, d, ff), BF16), pltpu.VMEM((e_loc, ff, d), BF16),
-                            pltpu.VMEM((n * cap, ff), BF16), pltpu.VMEM((n, rows, d), BF16),
-                            pltpu.VMEM((2, n, rows, d), BF16),
-                            dma((4,)), dma((2,)), dma((2,)), dma((2,)), dma, dma((2,)),
-                            dma((groups,)), dma((groups,)), dma((groups,)), dma((groups,)),
-                            dma((groups,)), dma((groups,)), dma, dma],
+                            dma((4,)), dma((2,)), dma((2,)), dma((2,)), dma((2,)), dma,
+                            dma((rounds,)), dma((rounds,)), dma((rounds,)), dma((rounds,)),
+                            dma((rounds,)), dma((rounds,)), dma, dma],
             compiler_params=pltpu.CompilerParams(collective_id=0, has_side_effects=True,
                                                  vmem_limit_bytes=67043328),
-        )(pad_mask, second_draw, jnp.transpose(choices, (0, 2, 1)), tokens,
-          norm_attn.reshape(1, d), norm_moe.reshape(1, d), w_gate.T, *turned, wo, w_in, w_out)
+        )(*operands)
+        out = lax.cond(flag[0, 0] > 0.5, full_layer, lambda: out)
         return out, loss[0, 0]
 
     by_group = P("ep")
     replicated = P()
-    in_specs = (by_group, by_group, by_group, by_group, replicated, replicated, replicated, replicated, replicated, replicated, replicated, by_group, by_group)
-    return jax.shard_map(local_step, mesh=mesh, in_specs=in_specs, out_specs=(by_group, replicated), check_vma=False)
+    placed = (by_group, by_group, by_group, by_group, replicated, replicated, replicated, replicated, replicated, replicated, replicated, by_group, by_group)
+    return jax.shard_map(local_step, mesh=mesh, in_specs=placed, out_specs=(by_group, replicated), check_vma=False)

time: 400 us -> 754 us (1.89)
  Pallas kernels: 384 us -> 736 us
    pallas_call x1 -> x2, Pallas kernels: 384 us -> 736 us  [the longest x1 381 us: full_layer(): pl.pallas_call(functools.partial(layer_kernel, n, heads, cap, groups), gr...]
where the time goes in v3:
time: 754 us; the launch traced here: 747 us
  Pallas kernels  736 us (98%)
  local copies, waits for them, and re-layouts  8.12 us (1%)
    pallas_call x1, Pallas kernels, full_layer(): pl.pallas_call(functools.partial(layer_kernel, n, heads, cap, groups), gr...  381 us
    pallas_call x1, Pallas kernels, local_step(): pl.pallas_call(functools.partial(packed_kernel, n, heads, cap, groups, s_...  355 us

profile of v3, /device:TPU:0, one launch (start us, length us, event | category | flops | bytes accessed | tf_op | source)
XLA Modules:
  0.0 747.0 jit_solution(1105946424810195053)
XLA Ops:
  0.6 354.9 %shard_map.140 = (bf16[16,256,1024]{2,1,0:T(8,128)(2,1)}, f32[1,1]{1,0:T(1,128)}, f32[1,1]{1,0:T(1,128)}, bf16[13,512,1024]{2,1,0:T(8,128)(2,1)}, bf16[13,512,1024]{2,1,0:T(8,128)(2,1)}) custom-call(s32[16,256]{1,0:T(8,128)} %mask_ref.1, f32[16,256]{1,0:T(8,128)} %draw_ref.1, s32[16,2,256]{2,1,0:T(2,128)} %bitcast.26, bf16[16,256,1024]{2,1,0:T(8,128)(2,1)} %tok_ref.1, ...), custom_call_target="tpu_custom_call" | custom-call | tf_op jit(solution)/shard_map/pallas_call | solution.py:648
  356.1 381.0 %conditional.1 = (bf16[16,256,1024]{2,1,0:T(8,128)(2,1)}) conditional(s32[]{:T(128)} %bitcast.11, bf16[16,256,1024]{2,1,0:T(8,128)(2,1)} %get-tuple-element.50, (s32[16,256]{1,0:T(8,128)}, f32[16,256]{1,0:T(8,128)}, s32[16,2,256]{2,1,0:T(2,128)}, bf16[16,256,1024]{2,1,0:T(8,128)(2,1)}, f32[1,1024]{1,0:T(1,128)}, /*index=5*/f32[1,1024]{1,0:T(1,128)}, ...), branch_computations={%region_0.0_spmd, %region_1.0_spmd} | conditional | bytes 8 | solution.py:670
  356.1 381.0 %branch_1_fun.1 = (bf16[16,256,1024]{2,1,0:T(8,128)(2,1)}, f32[1,1]{1,0:T(1,128)}, bf16[16,16,32,1024]{3,2,1,0:T(8,128)(2,1)}, bf16[16,16,32,1024]{3,2,1,0:T(8,128)(2,1)}) custom-call(s32[16,256]{1,0:T(8,128)} %get-tuple-element.30.mask_ref, f32[16,256]{1,0:T(8,128)} %get-tuple-element.31.draw_ref, s32[16,2,256]{2,1,0:T(2,128)} %get-tuple-element.32.pick_ref, ...), custom_call_target="tpu_custom_call" | custom-call | tf_op jit(solution)/shard_map/cond/branch_1_fun/pallas_call | solution.py:621
  737.1 8.1 %copy.19 = bf16[16,256,1024]{2,1,0:T(8,128)(2,1)} copy(bf16[16,256,1024]{2,1,0:T(8,128)(2,1)} %get-tuple-element.56) | data formatting | bytes 16777216
